TPU v7x, 32 devices: a whole 2x2x4 slice. The times are simulated.
32 devices in a mesh: ta: 2 (over x), gz: 4 (over y, core), gy: 4 (over z).
Axes of the slice: x: 2, y: 2, z: 4, core: 2. Of those that a mesh axis runs over, the one named last changes fastest.
Arguments:
- propagator: bfloat16 [2, 4, 3, 12, 2, 4, 512], P(None, None, None, None, 'ta', 'gz', 'gy'), may hold values from -6 to 6
- links: bfloat16 [2, 3, 3, 2, 4, 512], P(None, None, None, 'ta', 'gz', 'gy'), may hold values from -2.5 to 2.5
- source_z: int32 [2, 4], replicated, may hold values from 0 to 3
- displacements: int32 [3], replicated, may hold values from 0 to 2, each once
- momenta: int32 [4], replicated, may hold values from 1 to 3
- gamma_perm: int32 [4, 4], replicated, may hold values from 0 to 3, each once within a row
- gamma_phase: int32 [4, 4], replicated, may hold values from 0 to 3
Outputs:
- correlator: float32 [2, 3, 4, 4, 2], replicated
Inputs may be any that keep to these rules, and one draw needn't show every extreme that they name: `displacements`: every displacement from -1 to 1 appears exactly once. `gamma_perm`: each row is a permutation of the four spin indices.
All inputs are finite; a program needn't handle non-finite values.
Results may differ from a plain program's by a relative error of at most 0.0003.
Values may be sent and summed in bfloat16 or wider, within the bound.
No kernel may reach another device: no remote copies, remote signals or barrier semaphores. Data moves between devices by JAX's collectives and lax.ppermute only.
A program may use at most 64 MiB of HBM per device.

v0:
```python
import math

import jax
import jax.numpy as jnp
from jax import lax
from jax.sharding import PartitionSpec as P

highest = lax.Precision.HIGHEST


def from_behind(array, axis, by):
    peers = lax.axis_size(axis)
    return lax.ppermute(array, axis, [(i, (i + by) % peers) for i in range(peers)])


def colour_apply(wilson, field_now):
    left_real = wilson[0][None, :, :, None, :]
    left_imag = wilson[1][None, :, :, None, :]
    right_real = field_now[0][:, None, :, :, :]
    right_imag = field_now[1][:, None, :, :, :]
    real_part = jnp.sum(left_real * right_real - left_imag * right_imag, axis=2)
    imag_part = jnp.sum(left_real * right_imag + left_imag * right_real, axis=2)
    return jnp.stack([real_part, imag_part])


def link_product(left_link, right_link):
    left_real = left_link[0][:, :, None, :]
    left_imag = left_link[1][:, :, None, :]
    right_real = right_link[0][None, :, :, :]
    right_imag = right_link[1][None, :, :, :]
    real_part = jnp.sum(left_real * right_real - left_imag * right_imag, axis=1)
    imag_part = jnp.sum(left_real * right_imag + left_imag * right_real, axis=1)
    return jnp.stack([real_part, imag_part])


def spin_pairs(source, field_now):
    source_real = source[0][:, None]
    source_imag = source[1][:, None]
    field_real = field_now[0][None]
    field_imag = field_now[1][None]
    real_part = jnp.sum(source_real * field_real + source_imag * field_imag, axis=(2, 3))
    imag_part = jnp.sum(source_real * field_imag - source_imag * field_real, axis=(2, 3))
    return (real_part, imag_part)


def site_traces(gamma_real, gamma_imag, pairs):
    pair_real, pair_imag = pairs
    table_real = gamma_real[:, :, :, None]
    table_imag = gamma_imag[:, :, :, None]
    real_part = jnp.sum(table_real * pair_real[None] - table_imag * pair_imag[None], axis=(1, 2))
    imag_part = jnp.sum(table_real * pair_imag[None] + table_imag * pair_real[None], axis=(1, 2))
    return (real_part, imag_part)


def gamma_tables(gamma_perm, gamma_phase):
    columns = jnp.arange(4, dtype=jnp.int32)
    hits = (gamma_perm[:, :, None] == columns[None, None, :]).astype(jnp.float32)
    real_part = (gamma_phase == 0).astype(jnp.float32) - (gamma_phase == 2).astype(jnp.float32)
    imag_part = (gamma_phase == 1).astype(jnp.float32) - (gamma_phase == 3).astype(jnp.float32)
    return (hits * real_part[:, :, None], hits * imag_part[:, :, None])


def body(propagator, links, source_z, displacements, momenta, gamma_perm, gamma_phase):
    gamma_real, gamma_imag = gamma_tables(gamma_perm, gamma_phase)
    adjoint_real = jnp.swapaxes(gamma_real, 1, 2)
    adjoint_imag = -jnp.swapaxes(gamma_imag, 1, 2)
    depth_count = lax.axis_size("gz")
    nsteps = (displacements.shape[0] - 1) // 2
    slices_dev = propagator.shape[4]
    sites_dev = propagator.shape[6]
    slices_all = slices_dev * lax.axis_size("ta")
    sites_total = sites_dev * lax.axis_size("gy") * depth_count
    scaling = 1.0 / (24.0 * math.sqrt(sites_total))
    field_data, link_data = (propagator, links)
    depth_local = 1
    depth_start = lax.axis_index("gz")
    block_sites = field_data.shape[-1]
    line_length = depth_local * block_sites
    flat_length = slices_dev * line_length
    field_flat = jnp.reshape(field_data, (2, 4, 3, 12, flat_length))
    links_flat = jnp.reshape(link_data, (2, 3, 3, flat_length))
    positions = jnp.arange(flat_length, dtype=jnp.int32)
    depth_flat = depth_start + positions // block_sites % depth_local
    slice_flat = lax.axis_index("ta") * slices_dev + positions // line_length
    slice_ids = jnp.arange(slices_all, dtype=jnp.int32)
    slice_hits = slice_ids[:, None] == slice_flat[None, :]
    source_flat = jnp.sum(jnp.where(slice_hits[:, None, :], source_z[:, :, None], 0), axis=0)
    turn_count = momenta[:, None] * (depth_flat[None, :] - source_flat) % depth_count
    angles = turn_count.astype(jnp.float32) * (2.0 * math.pi / depth_count)
    cosine = jnp.cos(angles)
    sine_table = jnp.sin(angles)
    slice_weight = slice_hits.astype(jnp.float32)

    def contract(trace, table):
        return jnp.einsum("tl,gl,pl->tgp", slice_weight, trace, table, precision=highest)

    def project(traces):
        trace_real, trace_imag = traces
        real_part = contract(trace_real, cosine) + contract(trace_imag, sine_table)
        imag_part = contract(trace_imag, cosine) - contract(trace_real, sine_table)
        return jnp.stack([real_part, imag_part], axis=-1) * scaling

    source = field_flat.astype(jnp.float32)
    unit = jnp.broadcast_to(jnp.eye(3, dtype=jnp.float32)[:, :, None], (3, 3, flat_length))
    identity = jnp.stack([unit, jnp.zeros_like(unit)])
    results = {0: project(site_traces(gamma_real, gamma_imag, spin_pairs(source, source)))}
    wilson = identity
    moved_field = field_flat
    moved_links = links_flat
    for reach in range(1, nsteps + 1):
        wilson = link_product(wilson, moved_links.astype(jnp.float32))
        moved_field, moved_links = from_behind((moved_field, moved_links), "gz", -1)
        pairs = spin_pairs(source, colour_apply(wilson, moved_field.astype(jnp.float32)))
        results[reach] = project(site_traces(gamma_real, gamma_imag, pairs))
        mirrored_trace_real, mirrored_trace_imag = site_traces(adjoint_real, adjoint_imag, pairs)
        other_real = contract(mirrored_trace_real, cosine) - contract(
            mirrored_trace_imag, sine_table
        )
        other_imag = contract(mirrored_trace_imag, cosine) + contract(
            mirrored_trace_real, sine_table
        )
        shift_turn = momenta * reach % depth_count
        shift_angle = shift_turn.astype(jnp.float32) * (2.0 * math.pi / depth_count)
        shift_cos = jnp.cos(shift_angle)
        shift_sin = jnp.sin(shift_angle)
        mirrored_real_part = other_real * shift_cos - other_imag * shift_sin
        mirrored_imag_part = -other_imag * shift_cos - other_real * shift_sin
        results[-reach] = jnp.stack([mirrored_real_part, mirrored_imag_part], axis=-1) * scaling
    stacked = jnp.stack([results[offset] for offset in range(-nsteps, nsteps + 1)], axis=1)
    offsets = jnp.arange(2 * nsteps + 1, dtype=jnp.int32)
    select = (displacements[:, None] == offsets[None, :]).astype(jnp.float32)
    ordered = jnp.einsum("jl,tlgpc->tjgpc", select, stacked, precision=highest)
    return lax.psum(ordered, ("ta", "gz", "gy"))


def solution(mesh):
    placed = (
        P(None, None, None, None, "ta", "gz", "gy"),
        P(None, None, None, "ta", "gz", "gy"),
        P(),
        P(),
        P(),
        P(),
        P(),
    )
    return jax.shard_map(body, mesh=mesh, in_specs=placed, out_specs=P(), check_vma=False)
```

profile of v0, /device:TPU:0, one launch (start us, length us, event | category | flops | bytes accessed | tf_op | source)
XLA Modules:
  0.0 51.4 jit_solution(15262922463979435672)
XLA Ops:
  0.0 2.4 %collective-permute-start = (bf16[2,4,3,12,128]{4,1,3,2,0:T(4,128)(2,1)}, bf16[2,4,3,12,128]{4,1,3,2,0:T(4,128)(2,1)S(1)}, u32[]{:S(2)}, u32[]{:S(2)}) collective-permute-start(bf16[2,4,3,12,128]{4,1,3,2,0:T(4,128)(2,1)} %bitcast.123), channel_id=1, source_target_pairs={{0,12},{4,0},{8,4},{12,8},{1,13},{5,1},{9,5},{13,9},{2,14},{6,2},{... | collective-permute-start | bytes 221192 | tf_op jit(solution)/shard_map/ppermute | solution.py:13
  2.4 0.7 %copy_convert_fusion = f32[2,3,3,1,1,128]{5,2,1,4,3,0:T(4,128)S(1)} fusion(bf16[2,3,3,1,1,128]{5,0,4,3,2,1:T(2,128)(2,1)} %param.8), kind=kLoop, calls=%fused_computation.41 | loop fusion | flops 2304 | bytes 13824 | tf_op jit(solution)/shard_map/convert_element_type | solution.py:111
  3.1 0.9 %bitcast_convert_fusion = f32[2,4,3,12,128]{4,1,3,2,0:T(4,128)S(1)} fusion(bf16[2,4,3,12,1,1,128]{6,1,5,4,3,2,0:T(4,128)(2,1)} %param.7), kind=kLoop, calls=%fused_computation.140 | loop fusion | flops 36864 | bytes 221184 | tf_op jit(solution)/shard_map/convert_element_type | solution.py:103
  4.1 0.0 copy-start.1
  4.1 0.7 %copy-done.1 = s32[4,4]{1,0:T(4,128)S(1)} copy-done((s32[4,4]{1,0:T(4,128)S(1)}, s32[4,4]{1,0:T(4,128)}, u32[]{:S(2)}) %copy-start.1) | copy-done | bytes 88
  4.8 0.0 copy-start.3
  4.8 0.6 %copy-done.3 = s32[4]{0:T(128)S(1)} copy-done((s32[4]{0:T(128)S(1)}, s32[4]{0:T(128)}, u32[]{:S(2)}) %copy-start.3) | copy-done | bytes 40
  5.5 0.0 copy-start.2
  5.5 0.7 %copy-done.2 = s32[2,4]{1,0:T(2,128)S(1)} copy-done((s32[2,4]{1,0:T(2,128)S(1)}, s32[2,4]{1,0:T(2,128)}, u32[]{:S(2)}) %copy-start.2) | copy-done | bytes 56
  6.2 0.1 select_reduce_fusion
  6.3 0.1 fusion.88
  6.5 0.0 copy-start
  6.5 0.7 %copy-done = s32[4,4]{1,0:T(4,128)S(1)} copy-done((s32[4,4]{1,0:T(4,128)S(1)}, s32[4,4]{1,0:T(4,128)}, u32[]{:S(2)}) %copy-start) | copy-done | bytes 88
  7.2 0.1 fusion.6
  7.2 0.1 subtract_reduce_fusion.6
  7.3 0.0 collective-permute-done
  7.4 0.2 subtract_reduce_fusion.2
  7.6 0.4 add_reduce_fusion
  8.0 0.2 add_reduce_fusion.5
  8.1 0.2 fusion.24
  8.3 0.2 fusion.18
  8.5 0.2 convolution_add_fusion.1
  8.6 0.2 convolution_subtract_fusion.1
  8.8 0.2 fusion.34
  9.0 0.2 fusion.28
  9.1 0.2 convolution_subtract_fusion.2
  9.3 0.2 fusion.14
  9.4 0.2 fusion.8
  9.6 0.2 convolution_add_fusion
  9.8 0.2 convolution_subtract_fusion
  10.0 0.2 multiply_subtract_fusion.1
  10.2 0.0 copy-start.4
  10.2 0.6 %copy-done.4 = s32[3]{0:T(128)S(1)} copy-done((s32[3]{0:T(128)S(1)}, s32[3]{0:T(128)}, u32[]{:S(2)}) %copy-start.4) | copy-done | bytes 36
  10.8 0.2 convolution_bitcast_fusion
  11.1 39.7 %psum.7 = f32[2,3,4,4,2]{3,1,4,2,0:T(4,128)S(1)} all-reduce(f32[2,3,4,4,2]{3,1,4,2,0:T(4,128)S(1)} %convolution_bitcast_fusion), channel_id=1, replica_groups=mesh['ta'=2,'gz'=4,'gy'=4] {'ta','gz','gy'}, use_global_device_ids=true, to_apply=%region_15.16 | all-reduce | flops 192 | bytes 1536 | tf_op jit(solution)/shard_map/psum | solution.py:133
  50.8 0.6 %copy.45 = f32[2,3,4,4,2]{3,4,2,1,0:T(2,128)} copy(f32[2,3,4,4,2]{3,1,4,2,0:T(4,128)S(1)} %psum.7) | data formatting | bytes 1536 | tf_op jit(solution)/shard_map/psum | solution.py:133
  (16 shorter events, 0.3 us)
Async XLA Ops:
  0.0 7.3 %collective-permute-start = (bf16[2,4,3,12,128]{4,1,3,2,0:T(4,128)(2,1)}, bf16[2,4,3,12,128]{4,1,3,2,0:T(4,128)(2,1)S(1)}, u32[]{:S(2)}, u32[]{:S(2)}) collective-permute-start(bf16[2,4,3,12,128]{4,1,3,2,0:T(4,128)(2,1)} %bitcast.123), channel_id=1, source_target_pairs={{0,12},{4,0},{8,4},{12,8},{1,13},{5,1},{9,5},{13,9},{2,14},{6,2},{... | collective-permute-start | bytes 221192 | tf_op jit(solution)/shard_map/ppermute | solution.py:13
  4.1 0.7 %copy-start.1 = (s32[4,4]{1,0:T(4,128)S(1)}, s32[4,4]{1,0:T(4,128)}, u32[]{:S(2)}) copy-start(s32[4,4]{1,0:T(4,128)} %param.13) | copy-start | bytes 196
  4.8 0.7 %copy-start.3 = (s32[4]{0:T(128)S(1)}, s32[4]{0:T(128)}, u32[]{:S(2)}) copy-start(s32[4]{0:T(128)} %param.11) | copy-start | bytes 52
  5.5 0.7 %copy-start.2 = (s32[2,4]{1,0:T(2,128)S(1)}, s32[2,4]{1,0:T(2,128)}, u32[]{:S(2)}) copy-start(s32[2,4]{1,0:T(2,128)} %param.9) | copy-start | bytes 100
  6.5 0.7 %copy-start = (s32[4,4]{1,0:T(4,128)S(1)}, s32[4,4]{1,0:T(4,128)}, u32[]{:S(2)}) copy-start(s32[4,4]{1,0:T(4,128)} %param.12) | copy-start | bytes 196
  10.2 0.7 %copy-start.4 = (s32[3]{0:T(128)S(1)}, s32[3]{0:T(128)}, u32[]{:S(2)}) copy-start(s32[3]{0:T(128)} %param.10) | copy-start | bytes 40
where the time goes:
time: 51.7 us; the launch traced here: 51.4 us
  blocking collectives  39.7 us (77%)
  local copies, waits for them, and re-layouts  4.07 us (8%)
  other arithmetic  2.84 us (5%)
  starting transfers between devices  2.43 us (5%)
  matrix products  2.18 us (4%)
    psum x1, blocking collectives, body(): return lax.psum(ordered, ('ta', 'gz', 'gy'))  39.7 us
    unnamed x10, local copies, waits for them, and re-layouts  3.31 us
    ppermute x1, starting transfers between devices, from_behind(): lax.ppermute(array, axis, [(i, (i + by) % peers) for i in range(peers)])  2.43 us
    dot_general x12, matrix products, contract(): jnp.einsum('tl,gl,pl->tgp', slice_weight, trace, table, precision=highest)  1.96 us
  transfers between devices with their start and end apart: 1, of which 0 were waited for; matrix products, arithmetic and copies ran while one was open for 4% of the time, Pallas kernels for 0%

commit v1 on v0

v1 whole, which is shorter than its diff:
```python
import math

import jax
import jax.numpy as jnp
from jax import lax
from jax.experimental import pallas as pl
from jax.experimental.pallas import tpu as pltpu
from jax.sharding import PartitionSpec as P

f32 = jnp.float32
LANES = 128
PAD = 40


def vmem(count):
    return [pl.BlockSpec(memory_space=pltpu.VMEM) for _ in range(count)]


def smem(count):
    return [pl.BlockSpec(memory_space=pltpu.SMEM) for _ in range(count)]


def widen(packed_ref, wide_ref):
    rows = packed_ref.shape[0]
    wide_ref[0:rows, :] = packed_ref[...].astype(f32)
    wide_ref[rows:, :] = jnp.zeros((wide_ref.shape[0] - rows, wide_ref.shape[1]), f32)


def strided(wide_ref, part, spin, first, count, slices, now):
    start = ((part * 36 + first) * slices + now) * 4 + spin
    return wide_ref[pl.ds(start, count, stride=4 * slices), :]


def pair_sums(left_ref, wide_ref, slices, now, keep):
    for u in range(4):
        for s in range(4):
            real = imag = None
            for j in range(PAD // 8):
                rr = strided(wide_ref, 0, u, 8 * j, 8, slices, now)
                ri = strided(wide_ref, 1, u, 8 * j, 8, slices, now)
                lr = left_ref[pl.ds((now * 8 + s) * PAD + 8 * j, 8), :]
                li = left_ref[pl.ds((now * 8 + 4 + s) * PAD + 8 * j, 8), :]
                re = lr * rr - li * ri
                im = lr * ri + li * rr
                real = re if real is None else real + re
                imag = im if imag is None else imag + im
            keep(s, u, real, imag)


def left_rows(left_ref, now, part, s, first, value):
    left_ref[pl.ds((now * 8 + part * 4 + s) * PAD + first, value.shape[0]), :] = value


def dressed(left_ref, wide_ref, wilson, slices, now):
    zeros = jnp.zeros((PAD - 36, left_ref.shape[1]), f32)
    for s in range(4):
        for b in range(3):
            real = imag = None
            for a in range(3):
                sr = strided(wide_ref, 0, s, a * 12, 12, slices, now)
                si = strided(wide_ref, 1, s, a * 12, 12, slices, now)
                wr, wi = wilson(0, a, b), wilson(1, a, b)
                re = sr * wr + si * wi
                im = sr * wi - si * wr
                real = re if real is None else real + re
                imag = im if imag is None else imag + im
            left_rows(left_ref, now, 0, s, b * 12, real)
            left_rows(left_ref, now, 1, s, b * 12, imag)
        left_rows(left_ref, now, 0, s, 36, zeros)
        left_rows(left_ref, now, 1, s, 36, zeros)


def pairs_at(ref, now, s, u):
    base = now * 256 + (s * 4 + u) * 8
    return ref[pl.ds(pl.multiple_of(base, 8), 8), :], ref[pl.ds(pl.multiple_of(base + 128, 8), 8), :]


def keeper(ref, now):
    def keep(s, u, real, imag):
        ref[pl.ds(now * 256 + (s * 4 + u) * 8, 8), :] = real
        ref[pl.ds(now * 256 + 128 + (s * 4 + u) * 8, 8), :] = imag

    return keep


def first_kernel(slices, source_ref, links_ref, left_ref, pairs_ref, wilson_ref, wide_ref, plain_ref):
    widen(source_ref, wide_ref)
    for now in range(slices):
        zeros = jnp.zeros((PAD - 36, left_ref.shape[1]), f32)
        for s in range(4):
            left_rows(plain_ref, now, 0, s, 0, strided(wide_ref, 0, s, 0, 36, slices, now))
            left_rows(plain_ref, now, 1, s, 0, -strided(wide_ref, 1, s, 0, 36, slices, now))
            left_rows(plain_ref, now, 0, s, 36, zeros)
            left_rows(plain_ref, now, 1, s, 36, zeros)
        pair_sums(plain_ref, wide_ref, slices, now, keeper(pairs_ref, now))
        for part in range(2):
            for a in range(3):
                for b in range(3):
                    wilson_ref[pl.ds((now * 2 + part) * 9 + a * 3 + b, 1), :] = links_ref[a, b, now, part : part + 1, :].astype(f32)
        dressed(left_ref, wide_ref, lambda part, a, b: wilson_ref[pl.ds((now * 2 + part) * 9 + a * 3 + b, 1), :], slices, now)


def further_kernel(slices, source_ref, moved_ref, before_ref, left_ref, wilson_ref, wide_ref):
    widen(source_ref, wide_ref)
    for now in range(slices):
        def link(part, a, b):
            return moved_ref[a, b, now, part : part + 1, :].astype(f32)

        def old(part, a, b):
            return before_ref[pl.ds((now * 2 + part) * 9 + a * 3 + b, 1), :]

        for a in range(3):
            for b in range(3):
                real = sum(old(0, a, m) * link(0, m, b) - old(1, a, m) * link(1, m, b) for m in range(3))
                imag = sum(old(0, a, m) * link(1, m, b) + old(1, a, m) * link(0, m, b) for m in range(3))
                wilson_ref[pl.ds(now * 18 + a * 3 + b, 1), :] = real
                wilson_ref[pl.ds(now * 18 + 9 + a * 3 + b, 1), :] = imag
        dressed(left_ref, wide_ref, lambda part, a, b: wilson_ref[pl.ds((now * 2 + part) * 9 + a * 3 + b, 1), :], slices, now)


def pairs_kernel(slices, left_ref, moved_ref, pairs_ref, wide_ref):
    widen(moved_ref, wide_ref)
    for now in range(slices):
        pair_sums(left_ref, wide_ref, slices, now, keeper(pairs_ref, now))


def gamma_traces(pairs_ref, now, perm_ref, turn_ref, g, mirrored):
    real = imag = None
    for s in range(4):
        u = perm_ref[g, s]
        pr, pi = pairs_at(pairs_ref, now, u, s) if mirrored else pairs_at(pairs_ref, now, s, u)
        if mirrored:
            pi = -pi
        turn = turn_ref[g, s]
        cr = jnp.where(turn == 0, 1.0, jnp.where(turn == 2, -1.0, 0.0)).astype(f32)
        ci = jnp.where(turn == 1, 1.0, jnp.where(turn == 3, -1.0, 0.0)).astype(f32)
        re = cr * pr - ci * pi
        im = cr * pi + ci * pr
        real = re if real is None else real + re
        imag = im if imag is None else imag + im
    return jnp.sum(real, axis=0, keepdims=True), jnp.sum(imag, axis=0, keepdims=True)


def last_kernel(slices, nsteps, perm_ref, turn_ref, place_ref, left_ref, moved_ref, tables_ref, *rest):
    earlier, (out_ref, wide_ref, pairs_ref, real_ref, imag_ref) = rest[:nsteps], rest[nsteps:]
    widen(moved_ref, wide_ref)
    total = None
    rows = real_ref.shape[0]
    for now in range(slices):
        pair_sums(left_ref, wide_ref, slices, now, keeper(pairs_ref, now))
        real_ref[...] = jnp.zeros_like(real_ref)
        imag_ref[...] = jnp.zeros_like(imag_ref)
        for reach in range(nsteps + 1):
            source = pairs_ref if reach == nsteps else earlier[reach]
            for sign in (1, -1) if reach else (1,):
                for g in range(4):
                    re, im = gamma_traces(source, now, perm_ref, turn_ref, g, sign < 0)
                    row = place_ref[nsteps + sign * reach] * 4 + g
                    real_ref[pl.ds(row, 1), :] = re
                    imag_ref[pl.ds(row, 1), :] = im
        re = jnp.sum(real_ref[...], axis=1, keepdims=True)
        im = jnp.sum(imag_ref[...], axis=1, keepdims=True)
        part = re * tables_ref[now, 0] + im * tables_ref[now, 1]
        total = part if total is None else total + part
    out_ref[...] = total


def final_kernel(slices_all, entries, mine_ref, other_ref, out_ref):
    total = mine_ref[...] + other_ref[...]
    for t in range(slices_all):
        for c in range(2):
            for row in range(entries):
                at = t * 8 + c * 4
                out_ref[t, row // 4, row % 4, c : c + 1, :] = total[row : row + 1, at : at + 4]


def from_behind(array, axis, by):
    peers = lax.axis_size(axis)
    return lax.ppermute(array, axis, [(i, (i + by) % peers) for i in range(peers)])


def swap(array, mapping, sizes, axes):
    nt, nz, ny = sizes
    pairs = []
    for t in range(nt):
        for z in range(nz):
            for y in range(ny):
                a, b, c = mapping(t, z, y)
                pairs.append(((t * nz + z) * ny + y, (a * nz + b) * ny + c))
    return lax.ppermute(array, axes, pairs)


def body(propagator, links, source_z, displacements, momenta, gamma_perm, gamma_phase):
    axes = ("ta", "gz", "gy")
    sizes = tuple(lax.axis_size(a) for a in axes)
    depth_count = sizes[1]
    entries = displacements.shape[0]
    nsteps = (entries - 1) // 2
    slices = propagator.shape[4]
    sites = propagator.shape[6]
    slices_all = slices * sizes[0]
    scaling = 1.0 / (24.0 * math.sqrt(sites * sizes[2] * depth_count))
    source = jnp.reshape(jnp.transpose(propagator, (0, 2, 3, 4, 5, 1, 6)), (288 * slices, sites))
    linked = jnp.reshape(jnp.transpose(links, (1, 2, 3, 4, 0, 5)), (3, 3, slices, 2, sites))
    moved, moved_links = source, linked
    wide = pltpu.VMEM((288 * slices + 16 * slices, sites), f32)
    rows = -(-entries * 4 // 8) * 8

    depth = lax.axis_index("gz")
    first_slice = lax.axis_index("ta") * slices
    lane = jnp.arange(LANES, dtype=jnp.int32)
    lane_slice, lane_part, lane_p = lane // 8, (lane // 4) % 2, lane % 4
    hot_p = (lane_p[:, None] == jnp.arange(4)[None, :]).astype(jnp.int32)
    lane_mom = jnp.sum(hot_p * momenta[None, :], axis=1)
    hot_t = (lane_slice[:, None] == jnp.arange(slices_all)[None, :]).astype(jnp.int32)
    lane_src = jnp.sum(hot_t[:, :, None] * hot_p[:, None, :] * source_z[None, :, :], axis=(1, 2))
    row_entry = jnp.arange(rows, dtype=jnp.int32) // 4
    offset = jnp.sum((row_entry[:, None] == jnp.arange(entries)[None, :]).astype(jnp.int32) * displacements[None, :], axis=1) - nsteps
    ahead = jnp.maximum(-offset, 0)
    turn = lane_mom[None, :] * (depth + ahead[:, None] - lane_src[None, :]) % depth_count
    angle = turn.astype(f32) * (2.0 * math.pi / depth_count)
    cosine, sine = jnp.cos(angle) * scaling, jnp.sin(angle) * scaling
    first = jnp.where(lane_part == 0, cosine, -sine)
    second = jnp.where(lane_part == 0, sine, cosine)
    own = (lane_slice[None, :] == first_slice + jnp.arange(slices)[:, None]).astype(f32)
    tables = own[:, None, None, :] * jnp.stack([first, second])[None]
    place = jnp.sum((displacements[None, :] == jnp.arange(entries)[:, None]) * jnp.arange(entries, dtype=jnp.int32)[None, :], axis=1).astype(jnp.int32)

    moved = from_behind(moved, "gz", -1)
    shape_left = jax.ShapeDtypeStruct((slices * 8 * PAD, sites), f32)
    shape_pairs = jax.ShapeDtypeStruct((slices * 256, sites), f32)
    shape_wilson = jax.ShapeDtypeStruct((slices * 18, sites), f32)
    left, pairs, wilson = pl.pallas_call(
        lambda *refs: first_kernel(slices, *refs),
        out_shape=(shape_left, shape_pairs, shape_wilson),
        in_specs=vmem(2),
        out_specs=tuple(vmem(3)),
        scratch_shapes=[wide, pltpu.VMEM((slices * 8 * PAD, sites), f32)],
        name="local",
    )(source, linked)
    earlier = [pairs]
    for reach in range(1, nsteps):
        earlier.append(
            pl.pallas_call(
                lambda *refs: pairs_kernel(slices, *refs),
                out_shape=shape_pairs,
                in_specs=vmem(2),
                out_specs=vmem(1)[0],
                scratch_shapes=[wide],
                name="pairs",
            )(left, moved)
        )
        moved_links = from_behind(moved_links, "gz", -1)
        moved = from_behind(moved, "gz", -1)
        left, wilson = pl.pallas_call(
            lambda *refs: further_kernel(slices, *refs),
            out_shape=(shape_left, shape_wilson),
            in_specs=vmem(3),
            out_specs=tuple(vmem(2)),
            scratch_shapes=[wide],
            name="further",
        )(source, moved_links, wilson)
    total = pl.pallas_call(
        lambda *refs: last_kernel(slices, nsteps, *refs),
        out_shape=jax.ShapeDtypeStruct((rows, LANES), f32),
        in_specs=smem(3) + vmem(3 + nsteps),
        out_specs=vmem(1)[0],
        scratch_shapes=[wide, pltpu.VMEM((slices * 256, sites), f32), pltpu.VMEM((rows, sites), f32), pltpu.VMEM((rows, sites), f32)],
        name="last",
    )(gamma_perm, gamma_phase, place, left, moved, tables, *earlier)

    moves = []
    bit = 1
    while bit < sizes[1]:
        moves.append((0, bit, 0) if bit == 1 else (0, bit + 1, 0))
        bit *= 2
    for axis, size in ((0, sizes[0]), (2, sizes[2])):
        bit = 1
        while bit < size:
            moves.append(tuple(bit if a == axis else (1 if a == 1 else 0) for a in range(3)))
            bit *= 2
    received = None
    for t_bits, z_bits, y_bits in moves:
        if received is not None:
            total = total + received
        received = swap(total, lambda t, z, y: (t ^ t_bits, z ^ z_bits, y ^ y_bits), sizes, axes)
    out = pl.pallas_call(
        lambda *refs: final_kernel(slices_all, entries * 4, *refs),
        out_shape=jax.ShapeDtypeStruct((slices_all, entries, 4, 2, 4), f32),
        in_specs=vmem(2),
        name="final",
    )(total, received)
    return jnp.transpose(out, (0, 1, 2, 4, 3))


def solution(mesh):
    placed = (
        P(None, None, None, None, "ta", "gz", "gy"),
        P(None, None, None, "ta", "gz", "gy"),
        P(),
        P(),
        P(),
        P(),
        P(),
    )
    return jax.shard_map(body, mesh=mesh, in_specs=placed, out_specs=P(), check_vma=False)
```

time: 51.7 us -> 27.4 us (0.53)
  blocking collectives: 39.7 us -> 0 us
  waiting for transfers between devices: 0.01 us -> 8.94 us
  starting transfers between devices: 2.43 us -> 8.08 us
  Pallas kernels: 0 us -> 5.09 us
  matrix products: 2.18 us -> 0 us
  local copies, waits for them, and re-layouts: 4.07 us -> 2.53 us
    psum x1 -> x0, blocking collectives: 39.7 us -> none  [body(): return lax.psum(ordered, ('ta', 'gz', 'gy'))]
    ppermute x0 -> x5, waiting for transfers between devices: none -> 8.94 us  [swap(): return lax.ppermute(array, axes, pairs)]
    ppermute x0 -> x5, starting transfers between devices: none -> 5.65 us  [swap(): return lax.ppermute(array, axes, pairs)]
    pallas_call x0 -> x3, Pallas kernels: none -> 5.09 us  [the longest x1 1.94 us: body(): pl.pallas_call(lambda *refs: last_kernel(slices, nsteps, *refs), out_shap...]
    dot_general x13 -> x0, matrix products: 2.18 us -> none  [the longest x12 1.96 us: contract(): jnp.einsum('tl,gl,pl->tgp', slice_weight, trace, table, precision=highest)]
    convert_element_type x4 -> x3, other arithmetic: 1.61 us -> 0.01 us  [the longest x1 0.01 us: body(): (lane_slice[:, None] == jnp.arange(slices_all)[None, :]).astype(jnp.int32)]
    unnamed x10 -> x12, local copies, waits for them, and re-layouts: 3.31 us -> 2.53 us
    add x1 -> x5, other arithmetic: 0.01 us -> 0.72 us  [the longest x4 0.71 us: body(): total = total + received]
  transfers between devices with their start and end apart: 1 -> 6, of which waited for: 0 -> 5; matrix products, arithmetic and copies ran while one was open for 4% -> 6% of each run, Pallas kernels for 0% -> 6%
where the time goes in v1:
time: 27.4 us; the launch traced here: 27.1 us
  waiting for transfers between devices  8.94 us (33%)
  starting transfers between devices  8.08 us (29%)
  Pallas kernels  5.09 us (19%)
  local copies, waits for them, and re-layouts  2.53 us (9%)
  other arithmetic  2.37 us (9%)
    ppermute x5, waiting for transfers between devices, swap(): return lax.ppermute(array, axes, pairs)  8.94 us
    ppermute x5, starting transfers between devices, swap(): return lax.ppermute(array, axes, pairs)  5.65 us
    unnamed x12, local copies, waits for them, and re-layouts  2.53 us
    ppermute x1, starting transfers between devices, from_behind(): lax.ppermute(array, axis, [(i, (i + by) % peers) for i in range(peers)])  2.43 us
    pallas_call x1, Pallas kernels, body(): pl.pallas_call(lambda *refs: last_kernel(slices, nsteps, *refs), out_shap...  1.94 us
    pallas_call x1, Pallas kernels, body(): pl.pallas_call(lambda *refs: first_kernel(slices, *refs), out_shape=(shap...  1.75 us
    pallas_call x1, Pallas kernels, body(): pl.pallas_call(lambda *refs: final_kernel(slices_all, entries * 4, *refs)...  1.4 us
    add x4, other arithmetic, body(): total = total + received  0.71 us
  transfers between devices with their start and end apart: 6, of which 5 were waited for; matrix products, arithmetic and copies ran while one was open for 6% of the time, Pallas kernels for 6%

profile of v1, /device:TPU:0, one launch (start us, length us, event | category | flops | bytes accessed | tf_op | source)
XLA Modules:
  0.0 27.1 jit_solution(13852063086909817808)
XLA Ops:
  0.0 2.4 %collective-permute-start = (bf16[288,128]{1,0:T(8,128)(2,1)}, bf16[288,128]{1,0:T(8,128)(2,1)S(1)}, u32[]{:S(2)}, u32[]{:S(2)}) collective-permute-start(bf16[288,128]{1,0:T(8,128)(2,1)} %bitcast.13), channel_id=1, source_target_pairs={{0,12},{4,0},{8,4},{12,8},{1,13},{5,1},{9,5},{13,9},{2,14},{6,2},{... | collective-permute-start | bytes 221192 | tf_op jit(solution)/shard_map/ppermute | solution.py:179
  2.5 0.0 copy-start.4
  2.5 0.6 %copy-done.4 = s32[4]{0:T(128)S(1)} copy-done((s32[4]{0:T(128)S(1)}, s32[4]{0:T(128)}, u32[]{:S(2)}) %copy-start.4) | copy-done | bytes 40
  3.1 0.1 select_reduce_fusion.1
  3.2 0.0 copy-start.5
  3.2 1.8 %local.1 = (f32[320,128]{1,0:T(8,128)}, f32[256,128]{1,0:T(8,128)}, f32[18,128]{1,0:T(8,128)}) custom-call(bf16[288,128]{1,0:T(8,128)(2,1)} %bitcast.14, bf16[3,3,1,2,128]{4,3,2,1,0:T(2,128)(2,1)} %bitcast.15), custom_call_target="tpu_custom_call" | custom-call | tf_op jit(solution)/shard_map/local/pallas_call | solution.py:233
  5.0 0.0 copy-done.5
  5.0 0.1 select_reduce_fusion
  5.1 0.0 copy-start.3
  5.1 0.7 %copy-done.3 = s32[2,4]{1,0:T(2,128)S(1)} copy-done((s32[2,4]{1,0:T(2,128)S(1)}, s32[2,4]{1,0:T(2,128)}, u32[]{:S(2)}) %copy-start.3) | copy-done | bytes 56
  5.8 0.1 multiply_reduce_fusion
  5.8 0.1 select_bitcast_fusion.1
  6.0 0.6 %maximum_multiply_fusion.refs_5_ = f32[1,2,16,128]{3,2,1,0:T(8,128)} fusion(f32[1,1,16,128]{3,2,1,0:T(8,128)S(1)} %get-tuple-element.10, f32[1,1,16,128]{3,2,1,0:T(8,128)S(1)} %get-tuple-element.9, f32[128]{0:T(128)S(1)} %compare_convert_fusion.1), kind=kLoop, calls=%fused_computation | loop fusion | flops 8192 | bytes 33280 | tf_op jit(solution)/shard_map/mul | solution.py:226
  6.6 0.6 %select_reduce_fusion.2.refs_2_ = s32[3]{0:T(128)} fusion(s32[3]{0:T(128)S(1)} %copy-done.5), kind=kLoop, calls=%fused_computation.19 | loop fusion | flops 24 | bytes 24 | tf_op jit(solution)/shard_map/reduce_sum | solution.py:227
  7.2 0.0 collective-permute-done.refs_4_
  7.2 0.0 copy-start
  7.2 0.6 %copy-done = bf16[288,128]{1,0:T(8,128)(2,1)} copy-done((bf16[288,128]{1,0:T(8,128)(2,1)}, bf16[288,128]{1,0:T(8,128)(2,1)S(1)}, u32[]{:S(2)}) %copy-start) | copy-done | bytes 73752
  7.8 1.9 %last.1 = f32[16,128]{1,0:T(8,128)} custom-call(s32[4,4]{1,0:T(4,128)} %refs_0_.1, s32[4,4]{1,0:T(4,128)} %refs_1_.1, s32[3]{0:T(128)} %select_reduce_fusion.2.refs_2_, f32[320,128]{1,0:T(8,128)} %get-tuple-element.7.refs_3_, bf16[288,128]{1,0:T(8,128)(2,1)} %copy-done, f32[1,2,16,128]{3,2,1,0:T(8,128)} %maximum_multiply_fusion.refs_5_, ...), custom_call_target="tpu_custom_call" | custom-call | tf_op jit(solution)/shard_map/last/pallas_call | solution.py:263
  9.8 0.0 collective-permute-start.1
  9.8 1.4 %collective-permute-done.1 = f32[16,128]{1,0:T(8,128)S(1)} collective-permute-done((f32[16,128]{1,0:T(8,128)}, f32[16,128]{1,0:T(8,128)S(1)}, u32[]{:S(2)}, u32[]{:S(2)}) %collective-permute-start.1) | collective-permute-done | bytes 8224 | tf_op jit(solution)/shard_map/ppermute | solution.py:190
  11.2 0.7 %add.97 = f32[16,128]{1,0:T(8,128)S(1)} add(f32[16,128]{1,0:T(8,128)} %last.1, f32[16,128]{1,0:T(8,128)S(1)} %collective-permute-done.1) | non-fusion elementwise | flops 2048 | bytes 24576 | tf_op jit(solution)/shard_map/add | solution.py:285
  11.9 0.7 %collective-permute-start.2 = (f32[16,128]{1,0:T(8,128)S(1)}, f32[16,128]{1,0:T(8,128)S(1)}, u32[]{:S(2)}, u32[]{:S(2)}) collective-permute-start(f32[16,128]{1,0:T(8,128)S(1)} %add.97), channel_id=1, source_target_pairs={{0,12},{1,13},{2,14},{3,15},{4,8},{5,9},{6,10},{7,11},{8,4},{9,5},... | collective-permute-start | bytes 24584 | tf_op jit(solution)/shard_map/ppermute | solution.py:190
  12.5 2.4 %collective-permute-done.2 = f32[16,128]{1,0:T(8,128)S(1)} collective-permute-done((f32[16,128]{1,0:T(8,128)S(1)}, f32[16,128]{1,0:T(8,128)S(1)}, u32[]{:S(2)}, u32[]{:S(2)}) %collective-permute-start.2) | collective-permute-done | bytes 8224 | tf_op jit(solution)/shard_map/ppermute | solution.py:190
  14.9 1.3 %collective-permute-start.3 = (f32[16,128]{1,0:T(8,128)S(1)}, f32[16,128]{1,0:T(8,128)S(1)}, u32[]{:S(2)}, u32[]{:S(2)}) collective-permute-start(f32[16,128]{1,0:T(8,128)S(1)} %add.98), channel_id=1, source_target_pairs={{0,20},{1,21},{2,22},{3,23},{4,16},{5,17},{6,18},{7,19},{8,28},{9,... | collective-permute-start | bytes 24584 | tf_op jit(solution)/shard_map/ppermute | solution.py:190
  16.2 1.8 %collective-permute-done.3 = f32[16,128]{1,0:T(8,128)S(1)} collective-permute-done((f32[16,128]{1,0:T(8,128)S(1)}, f32[16,128]{1,0:T(8,128)S(1)}, u32[]{:S(2)}, u32[]{:S(2)}) %collective-permute-start.3) | collective-permute-done | bytes 8224 | tf_op jit(solution)/shard_map/ppermute | solution.py:190
  18.0 1.3 %collective-permute-start.4 = (f32[16,128]{1,0:T(8,128)S(1)}, f32[16,128]{1,0:T(8,128)S(1)}, u32[]{:S(2)}, u32[]{:S(2)}) collective-permute-start(f32[16,128]{1,0:T(8,128)S(1)} %add.99), channel_id=1, source_target_pairs={{0,5},{1,4},{2,7},{3,6},{4,1},{5,0},{6,3},{7,2},{8,13},{9,12},{10,... | collective-permute-start | bytes 24584 | tf_op jit(solution)/shard_map/ppermute | solution.py:190
  19.4 1.7 %collective-permute-done.4 = f32[16,128]{1,0:T(8,128)S(1)} collective-permute-done((f32[16,128]{1,0:T(8,128)S(1)}, f32[16,128]{1,0:T(8,128)S(1)}, u32[]{:S(2)}, u32[]{:S(2)}) %collective-permute-start.4) | collective-permute-done | bytes 8224 | tf_op jit(solution)/shard_map/ppermute | solution.py:190
  21.1 0.0 copy-start.1
  21.1 2.4 %collective-permute-start.5 = (f32[16,128]{1,0:T(8,128)S(1)}, f32[16,128]{1,0:T(8,128)S(1)}, u32[]{:S(2)}, u32[]{:S(2)}) collective-permute-start(f32[16,128]{1,0:T(8,128)S(1)} %add.100.refs_0_), channel_id=1, source_target_pairs={{0,6},{1,7},{2,4},{3,5},{4,2},{5,3},{6,0},{7,1},{8,14},{9,15},{10,... | collective-permute-start | bytes 24584 | tf_op jit(solution)/shard_map/ppermute | solution.py:190
  23.5 1.6 %collective-permute-done.5.refs_1_ = f32[16,128]{1,0:T(8,128)S(1)} collective-permute-done((f32[16,128]{1,0:T(8,128)S(1)}, f32[16,128]{1,0:T(8,128)S(1)}, u32[]{:S(2)}, u32[]{:S(2)}) %collective-permute-start.5) | collective-permute-done | bytes 8224 | tf_op jit(solution)/shard_map/ppermute | solution.py:190
  25.1 0.0 copy-done.1
  25.1 0.0 copy-start.2
  25.1 0.6 %copy-done.2 = f32[16,128]{1,0:T(8,128)} copy-done((f32[16,128]{1,0:T(8,128)}, f32[16,128]{1,0:T(8,128)S(1)}, u32[]{:S(2)}) %copy-start.2) | copy-done | bytes 8216
  25.7 1.4 %final.1 = f32[2,3,4,2,4]{4,3,2,1,0:T(2,128)} custom-call(f32[16,128]{1,0:T(8,128)} %copy-done.1, f32[16,128]{1,0:T(8,128)} %copy-done.2), custom_call_target="tpu_custom_call" | custom-call | tf_op jit(solution)/shard_map/final/pallas_call | solution.py:287
  (11 shorter events, 0.0 us)
Async XLA Ops:
  0.0 7.2 %collective-permute-start = (bf16[288,128]{1,0:T(8,128)(2,1)}, bf16[288,128]{1,0:T(8,128)(2,1)S(1)}, u32[]{:S(2)}, u32[]{:S(2)}) collective-permute-start(bf16[288,128]{1,0:T(8,128)(2,1)} %bitcast.13), channel_id=1, source_target_pairs={{0,12},{4,0},{8,4},{12,8},{1,13},{5,1},{9,5},{13,9},{2,14},{6,2},{... | collective-permute-start | bytes 221192 | tf_op jit(solution)/shard_map/ppermute | solution.py:179
  2.5 0.7 %copy-start.4 = (s32[4]{0:T(128)S(1)}, s32[4]{0:T(128)}, u32[]{:S(2)}) copy-start(s32[4]{0:T(128)} %param.11) | copy-start | bytes 52
  3.2 1.8 %copy-start.5 = (s32[3]{0:T(128)S(1)}, s32[3]{0:T(128)}, u32[]{:S(2)}) copy-start(s32[3]{0:T(128)} %param.10) | copy-start | bytes 40
  5.1 0.7 %copy-start.3 = (s32[2,4]{1,0:T(2,128)S(1)}, s32[2,4]{1,0:T(2,128)}, u32[]{:S(2)}) copy-start(s32[2,4]{1,0:T(2,128)} %param.9) | copy-start | bytes 100
  7.2 0.6 %copy-start = (bf16[288,128]{1,0:T(8,128)(2,1)}, bf16[288,128]{1,0:T(8,128)(2,1)S(1)}, u32[]{:S(2)}) copy-start(bf16[288,128]{1,0:T(8,128)(2,1)S(1)} %collective-permute-done.refs_4_) | copy-start | bytes 221188
  9.8 1.4 %collective-permute-start.1 = (f32[16,128]{1,0:T(8,128)}, f32[16,128]{1,0:T(8,128)S(1)}, u32[]{:S(2)}, u32[]{:S(2)}) collective-permute-start(f32[16,128]{1,0:T(8,128)} %last.1), channel_id=1, source_target_pairs={{0,4},{1,5},{2,6},{3,7},{4,0},{5,1},{6,2},{7,3},{8,12},{9,13},{10,... | collective-permute-start | bytes 24584 | tf_op jit(solution)/shard_map/ppermute | solution.py:190
  11.9 3.1 %collective-permute-start.2 = (f32[16,128]{1,0:T(8,128)S(1)}, f32[16,128]{1,0:T(8,128)S(1)}, u32[]{:S(2)}, u32[]{:S(2)}) collective-permute-start(f32[16,128]{1,0:T(8,128)S(1)} %add.97), channel_id=1, source_target_pairs={{0,12},{1,13},{2,14},{3,15},{4,8},{5,9},{6,10},{7,11},{8,4},{9,5},... | collective-permute-start | bytes 24584 | tf_op jit(solution)/shard_map/ppermute | solution.py:190
  14.9 3.1 %collective-permute-start.3 = (f32[16,128]{1,0:T(8,128)S(1)}, f32[16,128]{1,0:T(8,128)S(1)}, u32[]{:S(2)}, u32[]{:S(2)}) collective-permute-start(f32[16,128]{1,0:T(8,128)S(1)} %add.98), channel_id=1, source_target_pairs={{0,20},{1,21},{2,22},{3,23},{4,16},{5,17},{6,18},{7,19},{8,28},{9,... | collective-permute-start | bytes 24584 | tf_op jit(solution)/shard_map/ppermute | solution.py:190
  18.0 3.1 %collective-permute-start.4 = (f32[16,128]{1,0:T(8,128)S(1)}, f32[16,128]{1,0:T(8,128)S(1)}, u32[]{:S(2)}, u32[]{:S(2)}) collective-permute-start(f32[16,128]{1,0:T(8,128)S(1)} %add.99), channel_id=1, source_target_pairs={{0,5},{1,4},{2,7},{3,6},{4,1},{5,0},{6,3},{7,2},{8,13},{9,12},{10,... | collective-permute-start | bytes 24584 | tf_op jit(solution)/shard_map/ppermute | solution.py:190
  21.1 4.0 %copy-start.1 = (f32[16,128]{1,0:T(8,128)}, f32[16,128]{1,0:T(8,128)S(1)}, u32[]{:S(2)}) copy-start(f32[16,128]{1,0:T(8,128)S(1)} %add.100.refs_0_) | copy-start | bytes 24580
  21.1 4.0 %collective-permute-start.5 = (f32[16,128]{1,0:T(8,128)S(1)}, f32[16,128]{1,0:T(8,128)S(1)}, u32[]{:S(2)}, u32[]{:S(2)}) collective-permute-start(f32[16,128]{1,0:T(8,128)S(1)} %add.100.refs_0_), channel_id=1, source_target_pairs={{0,6},{1,7},{2,4},{3,5},{4,2},{5,3},{6,0},{7,1},{8,14},{9,15},{10,... | collective-permute-start | bytes 24584 | tf_op jit(solution)/shard_map/ppermute | solution.py:190
  25.1 0.6 %copy-start.2 = (f32[16,128]{1,0:T(8,128)}, f32[16,128]{1,0:T(8,128)S(1)}, u32[]{:S(2)}) copy-start(f32[16,128]{1,0:T(8,128)S(1)} %collective-permute-done.5.refs_1_) | copy-start | bytes 24580

commit v2 on v1

v2 whole, which is shorter than its diff:
```python
import math

import jax
import jax.numpy as jnp
from jax import lax
from jax.experimental import pallas as pl
from jax.experimental.pallas import tpu as pltpu
from jax.sharding import PartitionSpec as P

f32 = jnp.float32
LANES = 128
PAD = 40


def vmem(count):
    return [pl.BlockSpec(memory_space=pltpu.VMEM) for _ in range(count)]


def near(array):
    return pltpu.with_memory_space_constraint(array, pltpu.VMEM)


def kept(shape):
    return pltpu.VMEM(shape, f32)


def smem(count):
    return [pl.BlockSpec(memory_space=pltpu.SMEM) for _ in range(count)]


def widen(packed_ref, wide_ref):
    rows = packed_ref.shape[0]
    wide_ref[0:rows, :] = packed_ref[...].astype(f32)
    wide_ref[rows:, :] = jnp.zeros((wide_ref.shape[0] - rows, wide_ref.shape[1]), f32)


def strided(wide_ref, part, spin, first, count, slices, now):
    start = ((part * 36 + first) * slices + now) * 4 + spin
    return wide_ref[pl.ds(start, count, stride=4 * slices), :]


def pair_sums(left_ref, wide_ref, slices, now, keep):
    for u in range(4):
        for s in range(4):
            real = imag = None
            for j in range(PAD // 8):
                rr = strided(wide_ref, 0, u, 8 * j, 8, slices, now)
                ri = strided(wide_ref, 1, u, 8 * j, 8, slices, now)
                lr = left_ref[pl.ds((now * 8 + s) * PAD + 8 * j, 8), :]
                li = left_ref[pl.ds((now * 8 + 4 + s) * PAD + 8 * j, 8), :]
                re = lr * rr - li * ri
                im = lr * ri + li * rr
                real = re if real is None else real + re
                imag = im if imag is None else imag + im
            keep(s, u, real, imag)


def left_rows(left_ref, now, part, s, first, value):
    left_ref[pl.ds((now * 8 + part * 4 + s) * PAD + first, value.shape[0]), :] = value


def dressed(left_ref, wide_ref, wilson, slices, now):
    zeros = jnp.zeros((PAD - 36, left_ref.shape[1]), f32)
    for s in range(4):
        for b in range(3):
            real = imag = None
            for a in range(3):
                sr = strided(wide_ref, 0, s, a * 12, 12, slices, now)
                si = strided(wide_ref, 1, s, a * 12, 12, slices, now)
                wr, wi = wilson(0, a, b), wilson(1, a, b)
                re = sr * wr + si * wi
                im = sr * wi - si * wr
                real = re if real is None else real + re
                imag = im if imag is None else imag + im
            left_rows(left_ref, now, 0, s, b * 12, real)
            left_rows(left_ref, now, 1, s, b * 12, imag)
        left_rows(left_ref, now, 0, s, 36, zeros)
        left_rows(left_ref, now, 1, s, 36, zeros)


def keep_pairs(ref, now):
    def keep(s, u, real, imag):
        ref[pl.ds((s * 4 + u) * 8, 8), :] = real
        ref[pl.ds(128 + (s * 4 + u) * 8, 8), :] = imag

    return keep


def power_of_i(turn):
    real = jnp.where(turn == 0, 1.0, jnp.where(turn == 2, -1.0, 0.0)).astype(f32)
    imag = jnp.where(turn == 1, 1.0, jnp.where(turn == 3, -1.0, 0.0)).astype(f32)
    return real, imag


def tile_at(first):
    return pl.ds(first if isinstance(first, int) else pl.multiple_of(first, 8), 8)


def insert(plain_ref, left_ref, perm_ref, turn_ref, now):
    for g in range(4):
        for s in range(4):
            u = perm_ref[g, s]
            cr, ci = power_of_i(turn_ref[g, s])
            for mirrored in range(2):
                base = (now * 2 + mirrored) * 8 + g * 2
                taken, put, sign = (u, s, -1.0) if mirrored else (s, u, 1.0)
                for j in range(PAD // 8):
                    lr = plain_ref[tile_at((now * 8 + taken) * PAD + 8 * j), :]
                    li = plain_ref[tile_at((now * 8 + 4 + taken) * PAD + 8 * j), :]
                    left_ref[tile_at((base * 4 + put) * PAD + 8 * j), :] = cr * lr - (sign * ci) * li
                    left_ref[tile_at((base * 4 + 4 + put) * PAD + 8 * j), :] = cr * li + (sign * ci) * lr


def meet(left_ref, wide_ref, slices, now, rows_ref, first):
    sums = [None] * 16
    for u in range(4):
        for j in range(PAD // 8):
            rr = strided(wide_ref, 0, u, 8 * j, 8, slices, now)
            ri = strided(wide_ref, 1, u, 8 * j, 8, slices, now)
            for which in range(8):
                base = ((now * 16 + which * 2) * 4 + u) * PAD + 8 * j
                lr = left_ref[pl.ds(base, 8), :]
                li = left_ref[pl.ds(base + 4 * PAD, 8), :]
                re = lr * rr - li * ri
                im = lr * ri + li * rr
                at = (which // 4) * 8 + which % 4
                sums[at] = re if sums[at] is None else sums[at] + re
                sums[at + 4] = im if sums[at + 4] is None else sums[at + 4] + im
    for at in range(16):
        rows_ref[pl.ds(first + at, 1), :] = jnp.sum(sums[at], axis=0, keepdims=True)


def fill_tables(tables_ref, sizes, scaling, slices, entries, source_ref, entry_ref, momenta_ref):
    slices_all, depth_count = sizes
    nsteps = (entries - 1) // 2
    rows = tables_ref.shape[1]
    depth, first_slice = lax.axis_index("gz"), lax.axis_index("ta") * slices
    lane = lax.broadcasted_iota(jnp.int32, (8, LANES), 1)
    lane_slice, lane_part, lane_p = lane // 8, (lane // 4) % 2, lane % 4
    momentum = jnp.zeros((8, LANES), jnp.int32)
    origin = jnp.zeros((8, LANES), jnp.int32)
    for p in range(4):
        momentum = jnp.where(lane_p == p, momenta_ref[p], momentum)
        for t in range(slices_all):
            origin = jnp.where((lane_p == p) & (lane_slice == t), source_ref[t, p], origin)
    row = lax.broadcasted_iota(jnp.int32, (rows, LANES), 0)
    for l in range(entries):
        ahead = max(nsteps - l, 0)
        turn = lax.rem(momentum * (depth + ahead + depth_count - origin), depth_count)
        angle = turn.astype(f32) * (2.0 * math.pi / depth_count)
        cosine, sine = jnp.cos(angle) * scaling, jnp.sin(angle) * scaling
        first = jnp.where(lane_part == 0, cosine, -sine)
        second = jnp.where(lane_part == 0, sine, cosine)
        if l < nsteps:
            second = -second
        place = sum(jnp.where(entry_ref[j] == l, j, 0) for j in range(entries))
        for now in range(slices):
            own = lane_slice == first_slice + now
            for g in range(4):
                hit = row == place * 4 + g
                for which, table in ((0, first), (1, second)):
                    mine = jnp.where(own, table, 0.0)[0:1, :]
                    tables_ref[((now * entries + l) * 4 + g) * 2 + which] = jnp.where(hit, mine, 0.0)


def first_kernel(slices, sizes, scaling, entries, source_z_ref, entry_ref, momenta_ref, perm_ref, turn_ref, source_ref, links_ref,
                 left_ref, rows_ref, tables_ref, wilson_ref, wide_ref, plain_ref, pairs_ref):
    widen(source_ref, wide_ref)
    fill_tables(tables_ref, sizes, scaling, slices, entries, source_z_ref, entry_ref, momenta_ref)
    zeros = jnp.zeros((PAD - 36, LANES), f32)
    for now in range(slices):
        for s in range(4):
            left_rows(plain_ref, now, 0, s, 0, strided(wide_ref, 0, s, 0, 36, slices, now))
            left_rows(plain_ref, now, 1, s, 0, -strided(wide_ref, 1, s, 0, 36, slices, now))
            left_rows(plain_ref, now, 0, s, 36, zeros)
            left_rows(plain_ref, now, 1, s, 36, zeros)
        pair_sums(plain_ref, wide_ref, slices, now, keep_pairs(pairs_ref, now))
        for g in range(4):
            real = imag = None
            for s in range(4):
                at = (s * 4 + perm_ref[g, s]) * 8
                pr, pi = pairs_ref[tile_at(at), :], pairs_ref[tile_at(at + 128), :]
                cr, ci = power_of_i(turn_ref[g, s])
                re, im = cr * pr - ci * pi, cr * pi + ci * pr
                real = re if real is None else real + re
                imag = im if imag is None else imag + im
            rows_ref[now * 8 + g : now * 8 + g + 1, :] = jnp.sum(real, axis=0, keepdims=True)
            rows_ref[now * 8 + 4 + g : now * 8 + 5 + g, :] = jnp.sum(imag, axis=0, keepdims=True)
        for part in range(2):
            for a in range(3):
                for b in range(3):
                    wilson_ref[pl.ds((now * 2 + part) * 9 + a * 3 + b, 1), :] = links_ref[a, b, now, part : part + 1, :].astype(f32)
        dressed(plain_ref, wide_ref, lambda part, a, b: wilson_ref[pl.ds((now * 2 + part) * 9 + a * 3 + b, 1), :], slices, now)
        insert(plain_ref, left_ref, perm_ref, turn_ref, now)


def further_kernel(slices, perm_ref, turn_ref, source_ref, moved_ref, before_ref, left_ref, wilson_ref, wide_ref, plain_ref):
    widen(source_ref, wide_ref)
    for now in range(slices):
        def link(part, a, b):
            return moved_ref[a, b, now, part : part + 1, :].astype(f32)

        def old(part, a, b):
            return before_ref[pl.ds((now * 2 + part) * 9 + a * 3 + b, 1), :]

        for a in range(3):
            for b in range(3):
                real = sum(old(0, a, m) * link(0, m, b) - old(1, a, m) * link(1, m, b) for m in range(3))
                imag = sum(old(0, a, m) * link(1, m, b) + old(1, a, m) * link(0, m, b) for m in range(3))
                wilson_ref[pl.ds(now * 18 + a * 3 + b, 1), :] = real
                wilson_ref[pl.ds(now * 18 + 9 + a * 3 + b, 1), :] = imag
        dressed(plain_ref, wide_ref, lambda part, a, b: wilson_ref[pl.ds((now * 2 + part) * 9 + a * 3 + b, 1), :], slices, now)
        insert(plain_ref, left_ref, perm_ref, turn_ref, now)


def middle_kernel(slices, left_ref, moved_ref, rows_ref, wide_ref):
    widen(moved_ref, wide_ref)
    for now in range(slices):
        meet(left_ref, wide_ref, slices, now, rows_ref, now * 16)


def last_kernel(slices, nsteps, left_ref, moved_ref, tables_ref, *rest):
    earlier, (out_ref, wide_ref, rows_ref) = rest[:nsteps], rest[nsteps:]
    widen(moved_ref, wide_ref)
    total = None
    entries = 2 * nsteps + 1
    for now in range(slices):
        rows_ref[nsteps * 8 : nsteps * 8 + 8, :] = earlier[0][now * 8 : now * 8 + 8, :]
        for reach in range(1, nsteps):
            rows_ref[(nsteps + reach) * 8 : (nsteps + reach) * 8 + 8, :] = earlier[reach][now * 16 : now * 16 + 8, :]
            rows_ref[(nsteps - reach) * 8 : (nsteps - reach) * 8 + 8, :] = earlier[reach][now * 16 + 8 : now * 16 + 16, :]
        meet(left_ref, wide_ref, slices, now, rows_ref, entries * 8)
        rows_ref[2 * nsteps * 8 : entries * 8, :] = rows_ref[entries * 8 : entries * 8 + 8, :]
        rows_ref[0:8, :] = rows_ref[entries * 8 + 8 : entries * 8 + 16, :]
        summed = jnp.sum(rows_ref[0 : entries * 8, :], axis=1, keepdims=True)
        rows_ref[0 : entries * 8, :] = jnp.broadcast_to(summed, (entries * 8, LANES))
        for l in range(entries):
            for g in range(4):
                at = ((now * entries + l) * 4 + g) * 2
                part = rows_ref[l * 8 + g : l * 8 + g + 1, :] * tables_ref[at] + rows_ref[l * 8 + 4 + g : l * 8 + 5 + g, :] * tables_ref[at + 1]
                total = part if total is None else total + part
    out_ref[...] = total


def final_kernel(slices_all, entries, mine_ref, other_ref, out_ref):
    total = mine_ref[...] + other_ref[...]
    for t in range(slices_all):
        for c in range(2):
            for row in range(entries):
                at = t * 8 + c * 4
                out_ref[t, row // 4, row % 4, c : c + 1, :] = total[row : row + 1, at : at + 4]


def from_behind(array, axis, by):
    peers = lax.axis_size(axis)
    return lax.ppermute(array, axis, [(i, (i + by) % peers) for i in range(peers)])


def swap(array, mapping, sizes, axes):
    nt, nz, ny = sizes
    pairs = []
    for t in range(nt):
        for z in range(nz):
            for y in range(ny):
                a, b, c = mapping(t, z, y)
                pairs.append(((t * nz + z) * ny + y, (a * nz + b) * ny + c))
    return lax.ppermute(array, axes, pairs)


def body(propagator, links, source_z, displacements, momenta, gamma_perm, gamma_phase):
    axes = ("ta", "gz", "gy")
    sizes = tuple(lax.axis_size(a) for a in axes)
    depth_count = sizes[1]
    entries = displacements.shape[0]
    nsteps = (entries - 1) // 2
    slices = propagator.shape[4]
    sites = propagator.shape[6]
    slices_all = slices * sizes[0]
    scaling = 1.0 / (24.0 * math.sqrt(sites * sizes[2] * depth_count))
    source = jnp.reshape(jnp.transpose(propagator, (0, 2, 3, 4, 5, 1, 6)), (288 * slices, sites))
    linked = jnp.reshape(jnp.transpose(links, (1, 2, 3, 4, 0, 5)), (3, 3, slices, 2, sites))
    moved, moved_links = source, linked
    wide = pltpu.VMEM((288 * slices + 16 * slices, sites), f32)
    plain = pltpu.VMEM((slices * 8 * PAD, sites), f32)
    rows = -(-entries * 4 // 8) * 8

    moved = from_behind(moved, "gz", -1)
    shape_left = kept((slices * 64 * PAD, sites))
    shape_wilson = kept((slices * 18, sites))
    left, first_rows, tables, wilson = pl.pallas_call(
        lambda *refs: first_kernel(slices, (slices_all, depth_count), scaling, entries, *refs),
        out_shape=(shape_left, kept((slices * 8, sites)), kept((slices * entries * 8, rows, LANES)), shape_wilson),
        in_specs=smem(5) + vmem(2),
        out_specs=tuple(vmem(4)),
        scratch_shapes=[wide, plain, pltpu.VMEM((256, sites), f32)],
        name="local",
    )(source_z, displacements, momenta, gamma_perm, gamma_phase, source, linked)
    earlier = [first_rows]
    for reach in range(1, nsteps):
        earlier.append(
            pl.pallas_call(
                lambda *refs: middle_kernel(slices, *refs),
                out_shape=kept((slices * 16, sites)),
                in_specs=vmem(2),
                out_specs=vmem(1)[0],
                scratch_shapes=[wide],
                name="middle",
            )(near(left), near(moved))
        )
        moved_links = from_behind(moved_links, "gz", -1)
        moved = from_behind(moved, "gz", -1)
        left, wilson = pl.pallas_call(
            lambda *refs: further_kernel(slices, *refs),
            out_shape=(shape_left, shape_wilson),
            in_specs=smem(2) + vmem(3),
            out_specs=tuple(vmem(2)),
            scratch_shapes=[wide, plain],
            name="further",
        )(gamma_perm, gamma_phase, source, moved_links, near(wilson))
    total = pl.pallas_call(
        lambda *refs: last_kernel(slices, nsteps, *refs),
        out_shape=kept((rows, LANES)),
        in_specs=vmem(3 + nsteps),
        out_specs=vmem(1)[0],
        scratch_shapes=[wide, pltpu.VMEM((entries * 8 + 16, sites), f32)],
        name="last",
    )(near(left), near(moved), near(tables), *(near(e) for e in earlier))

    moves = []
    bit = 1
    while bit < sizes[1]:
        moves.append((0, bit, 0) if bit == 1 else (0, bit + 1, 0))
        bit *= 2
    for axis, size in ((0, sizes[0]), (2, sizes[2])):
        bit = 1
        while bit < size:
            moves.append(tuple(bit if a == axis else (1 if a == 1 else 0) for a in range(3)))
            bit *= 2
    received = None
    for t_bits, z_bits, y_bits in moves:
        if received is not None:
            total = total + received
        received = swap(total, lambda t, z, y: (t ^ t_bits, z ^ z_bits, y ^ y_bits), sizes, axes)
    out = pl.pallas_call(
        lambda *refs: final_kernel(slices_all, entries * 4, *refs),
        out_shape=jax.ShapeDtypeStruct((slices_all, entries, 4, 2, 4), f32),
        in_specs=vmem(2),
        name="final",
    )(near(total), near(received))
    return jnp.transpose(out, (0, 1, 2, 4, 3))


def solution(mesh):
    placed = (
        P(None, None, None, None, "ta", "gz", "gy"),
        P(None, None, None, "ta", "gz", "gy"),
        P(),
        P(),
        P(),
        P(),
        P(),
    )
    return jax.shard_map(body, mesh=mesh, in_specs=placed, out_specs=P(), check_vma=False)
```

time: 27.4 us -> 20.5 us (0.75)
  local copies, waits for them, and re-layouts: 2.53 us -> 0 us
  other arithmetic: 2.37 us -> 0.01 us
  Pallas kernels: 5.09 us -> 2.83 us
  starting transfers between devices: 8.08 us -> 9.97 us
  waiting for transfers between devices: 8.94 us -> 7.57 us
    unnamed x12 -> x0, local copies, waits for them, and re-layouts: 2.53 us -> none
    ppermute x5, starting transfers between devices: 5.65 us -> 7.54 us  [swap(): return lax.ppermute(array, axes, pairs)]
    ppermute x5, waiting for transfers between devices: 8.94 us -> 7.12 us  [swap(): return lax.ppermute(array, axes, pairs)]
    pallas_call x1, Pallas kernels: 1.94 us -> 0.29 us  [body(): pl.pallas_call(lambda *refs: last_kernel(slices, nsteps, *refs), out_shap...]
    reduce_sum x4 -> x0, other arithmetic: 0.88 us -> none  [the longest x1 0.63 us: body(): jnp.sum((displacements[None, :] == jnp.arange(entries)[:, None]) * jnp.ar...]
    pallas_call x1, Pallas kernels: 1.4 us -> 0.69 us  [body(): pl.pallas_call(lambda *refs: final_kernel(slices_all, entries * 4, *refs)...]
    add x4, other arithmetic: 0.71 us -> 0.01 us  [body(): total = total + received]
    mul x1 -> x0, other arithmetic: 0.61 us -> none  [body(): tables = own[:, None, None, :] * jnp.stack([first, second])[None]]
  transfers between devices with their start and end apart: 6 -> 6, of which waited for: 5 -> 6; matrix products, arithmetic and copies ran while one was open for 6% -> 0% of each run, Pallas kernels for 6% -> 9%
where the time goes in v2:
time: 20.5 us; the launch traced here: 20.4 us
  starting transfers between devices  9.97 us (49%)
  waiting for transfers between devices  7.57 us (37%)
  Pallas kernels  2.83 us (14%)
    ppermute x5, starting transfers between devices, swap(): return lax.ppermute(array, axes, pairs)  7.54 us
    ppermute x5, waiting for transfers between devices, swap(): return lax.ppermute(array, axes, pairs)  7.12 us
    ppermute x1, starting transfers between devices, from_behind(): lax.ppermute(array, axis, [(i, (i + by) % peers) for i in range(peers)])  2.43 us
    pallas_call x1, Pallas kernels, body(): pl.pallas_call(lambda *refs: first_kernel(slices, (slices_all, depth_coun...  1.85 us
    pallas_call x1, Pallas kernels, body(): pl.pallas_call(lambda *refs: final_kernel(slices_all, entries * 4, *refs)...  0.69 us
    ppermute x1, waiting for transfers between devices, from_behind(): lax.ppermute(array, axis, [(i, (i + by) % peers) for i in range(peers)])  0.45 us
  transfers between devices with their start and end apart: 6, of which 6 were waited for; matrix products, arithmetic and copies ran while one was open for 0% of the time, Pallas kernels for 9%

profile of v2, /device:TPU:0, one launch (start us, length us, event | category | flops | bytes accessed | tf_op | source)
XLA Modules:
  0.0 20.4 jit_solution(14459310423661739241)
XLA Ops:
  0.0 2.4 %collective-permute-start = (bf16[288,128]{1,0:T(8,128)(2,1)}, bf16[288,128]{1,0:T(8,128)(2,1)S(1)}, u32[]{:S(2)}, u32[]{:S(2)}) collective-permute-start(bf16[288,128]{1,0:T(8,128)(2,1)} %bitcast.9), channel_id=1, source_target_pairs={{0,12},{4,0},{8,4},{12,8},{1,13},{5,1},{9,5},{13,9},{2,14},{6,2},{... | collective-permute-start | bytes 221192 | tf_op jit(solution)/shard_map/ppermute | solution.py:256
  2.4 1.9 %local.1 = (f32[2560,128]{1,0:T(8,128)S(1)}, f32[8,128]{1,0:T(8,128)S(1)}, f32[24,16,128]{2,1,0:T(8,128)S(1)}, f32[18,128]{1,0:T(8,128)}) custom-call(s32[2,4]{1,0:T(2,128)} %refs_0_.1, s32[3]{0:T(128)} %refs_1_.1, s32[4]{0:T(128)} %refs_2_.1, s32[4,4]{1,0:T(4,128)} %refs_3_.1, s32[4,4]{1,0:T(4,128)} %refs_4_.1, bf16[288,128]{1,0:T(8,128)(2,1)} %bitcast.10, ...), custom_call_target="tpu_custom_call" | custom-call | tf_op jit(solution)/shard_map/local/pallas_call | solution.py:290
  4.3 0.4 %collective-permute-done.refs_1_ = bf16[288,128]{1,0:T(8,128)(2,1)S(1)} collective-permute-done((bf16[288,128]{1,0:T(8,128)(2,1)}, bf16[288,128]{1,0:T(8,128)(2,1)S(1)}, u32[]{:S(2)}, u32[]{:S(2)}) %collective-permute-start) | collective-permute-done | bytes 73760 | tf_op jit(solution)/shard_map/ppermute | solution.py:256
  4.7 0.3 %last.1 = f32[16,128]{1,0:T(8,128)S(1)} custom-call(f32[2560,128]{1,0:T(8,128)S(1)} %get-tuple-element.8.refs_0_, bf16[288,128]{1,0:T(8,128)(2,1)S(1)} %collective-permute-done.refs_1_, f32[24,16,128]{2,1,0:T(8,128)S(1)} %get-tuple-element.9.refs_2_, f32[8,128]{1,0:T(8,128)S(1)} %get-tuple-element.10.refs_3_), custom_call_target="tpu_custom_call" | custom-call | tf_op jit(solution)/shard_map/last/pallas_call | solution.py:320
  5.0 0.6 %collective-permute-start.1 = (f32[16,128]{1,0:T(8,128)S(1)}, f32[16,128]{1,0:T(8,128)S(1)}, u32[]{:S(2)}, u32[]{:S(2)}) collective-permute-start(f32[16,128]{1,0:T(8,128)S(1)} %last.1), channel_id=1, source_target_pairs={{0,4},{1,5},{2,6},{3,7},{4,0},{5,1},{6,2},{7,3},{8,12},{9,13},{10,... | collective-permute-start | bytes 24584 | tf_op jit(solution)/shard_map/ppermute | solution.py:267
  5.7 0.8 %collective-permute-done.1 = f32[16,128]{1,0:T(8,128)S(1)} collective-permute-done((f32[16,128]{1,0:T(8,128)S(1)}, f32[16,128]{1,0:T(8,128)S(1)}, u32[]{:S(2)}, u32[]{:S(2)}) %collective-permute-start.1) | collective-permute-done | bytes 8224 | tf_op jit(solution)/shard_map/ppermute | solution.py:267
  6.5 1.4 %collective-permute-start.2 = (f32[16,128]{1,0:T(8,128)S(1)}, f32[16,128]{1,0:T(8,128)S(1)}, u32[]{:S(2)}, u32[]{:S(2)}) collective-permute-start(f32[16,128]{1,0:T(8,128)S(1)} %add.12), channel_id=1, source_target_pairs={{0,12},{1,13},{2,14},{3,15},{4,8},{5,9},{6,10},{7,11},{8,4},{9,5},... | collective-permute-start | bytes 24584 | tf_op jit(solution)/shard_map/ppermute | solution.py:267
  7.9 1.7 %collective-permute-done.2 = f32[16,128]{1,0:T(8,128)S(1)} collective-permute-done((f32[16,128]{1,0:T(8,128)S(1)}, f32[16,128]{1,0:T(8,128)S(1)}, u32[]{:S(2)}, u32[]{:S(2)}) %collective-permute-start.2) | collective-permute-done | bytes 8224 | tf_op jit(solution)/shard_map/ppermute | solution.py:267
  9.6 1.4 %collective-permute-start.3 = (f32[16,128]{1,0:T(8,128)S(1)}, f32[16,128]{1,0:T(8,128)S(1)}, u32[]{:S(2)}, u32[]{:S(2)}) collective-permute-start(f32[16,128]{1,0:T(8,128)S(1)} %add.13), channel_id=1, source_target_pairs={{0,20},{1,21},{2,22},{3,23},{4,16},{5,17},{6,18},{7,19},{8,28},{9,... | collective-permute-start | bytes 24584 | tf_op jit(solution)/shard_map/ppermute | solution.py:267
  11.0 1.6 %collective-permute-done.3 = f32[16,128]{1,0:T(8,128)S(1)} collective-permute-done((f32[16,128]{1,0:T(8,128)S(1)}, f32[16,128]{1,0:T(8,128)S(1)}, u32[]{:S(2)}, u32[]{:S(2)}) %collective-permute-start.3) | collective-permute-done | bytes 8224 | tf_op jit(solution)/shard_map/ppermute | solution.py:267
  12.6 1.5 %collective-permute-start.4 = (f32[16,128]{1,0:T(8,128)S(1)}, f32[16,128]{1,0:T(8,128)S(1)}, u32[]{:S(2)}, u32[]{:S(2)}) collective-permute-start(f32[16,128]{1,0:T(8,128)S(1)} %add.14), channel_id=1, source_target_pairs={{0,5},{1,4},{2,7},{3,6},{4,1},{5,0},{6,3},{7,2},{8,13},{9,12},{10,... | collective-permute-start | bytes 24584 | tf_op jit(solution)/shard_map/ppermute | solution.py:267
  14.2 1.6 %collective-permute-done.4 = f32[16,128]{1,0:T(8,128)S(1)} collective-permute-done((f32[16,128]{1,0:T(8,128)S(1)}, f32[16,128]{1,0:T(8,128)S(1)}, u32[]{:S(2)}, u32[]{:S(2)}) %collective-permute-start.4) | collective-permute-done | bytes 8224 | tf_op jit(solution)/shard_map/ppermute | solution.py:267
  15.7 2.5 %collective-permute-start.5 = (f32[16,128]{1,0:T(8,128)S(1)}, f32[16,128]{1,0:T(8,128)S(1)}, u32[]{:S(2)}, u32[]{:S(2)}) collective-permute-start(f32[16,128]{1,0:T(8,128)S(1)} %add.15.refs_0_), channel_id=1, source_target_pairs={{0,6},{1,7},{2,4},{3,5},{4,2},{5,3},{6,0},{7,1},{8,14},{9,15},{10,... | collective-permute-start | bytes 24584 | tf_op jit(solution)/shard_map/ppermute | solution.py:267
  18.3 1.4 %collective-permute-done.5.refs_1_ = f32[16,128]{1,0:T(8,128)S(1)} collective-permute-done((f32[16,128]{1,0:T(8,128)S(1)}, f32[16,128]{1,0:T(8,128)S(1)}, u32[]{:S(2)}, u32[]{:S(2)}) %collective-permute-start.5) | collective-permute-done | bytes 8224 | tf_op jit(solution)/shard_map/ppermute | solution.py:267
  19.7 0.7 %final.1 = f32[2,3,4,2,4]{4,3,2,1,0:T(2,128)} custom-call(f32[16,128]{1,0:T(8,128)S(1)} %add.15.refs_0_, f32[16,128]{1,0:T(8,128)S(1)} %collective-permute-done.5.refs_1_), custom_call_target="tpu_custom_call" | custom-call | tf_op jit(solution)/shard_map/final/pallas_call | solution.py:344
  (4 shorter events, 0.0 us)
Async XLA Ops:
  0.0 4.7 %collective-permute-start = (bf16[288,128]{1,0:T(8,128)(2,1)}, bf16[288,128]{1,0:T(8,128)(2,1)S(1)}, u32[]{:S(2)}, u32[]{:S(2)}) collective-permute-start(bf16[288,128]{1,0:T(8,128)(2,1)} %bitcast.9), channel_id=1, source_target_pairs={{0,12},{4,0},{8,4},{12,8},{1,13},{5,1},{9,5},{13,9},{2,14},{6,2},{... | collective-permute-start | bytes 221192 | tf_op jit(solution)/shard_map/ppermute | solution.py:256
  5.0 1.5 %collective-permute-start.1 = (f32[16,128]{1,0:T(8,128)S(1)}, f32[16,128]{1,0:T(8,128)S(1)}, u32[]{:S(2)}, u32[]{:S(2)}) collective-permute-start(f32[16,128]{1,0:T(8,128)S(1)} %last.1), channel_id=1, source_target_pairs={{0,4},{1,5},{2,6},{3,7},{4,0},{5,1},{6,2},{7,3},{8,12},{9,13},{10,... | collective-permute-start | bytes 24584 | tf_op jit(solution)/shard_map/ppermute | solution.py:267
  6.5 3.1 %collective-permute-start.2 = (f32[16,128]{1,0:T(8,128)S(1)}, f32[16,128]{1,0:T(8,128)S(1)}, u32[]{:S(2)}, u32[]{:S(2)}) collective-permute-start(f32[16,128]{1,0:T(8,128)S(1)} %add.12), channel_id=1, source_target_pairs={{0,12},{1,13},{2,14},{3,15},{4,8},{5,9},{6,10},{7,11},{8,4},{9,5},... | collective-permute-start | bytes 24584 | tf_op jit(solution)/shard_map/ppermute | solution.py:267
  9.6 3.1 %collective-permute-start.3 = (f32[16,128]{1,0:T(8,128)S(1)}, f32[16,128]{1,0:T(8,128)S(1)}, u32[]{:S(2)}, u32[]{:S(2)}) collective-permute-start(f32[16,128]{1,0:T(8,128)S(1)} %add.13), channel_id=1, source_target_pairs={{0,20},{1,21},{2,22},{3,23},{4,16},{5,17},{6,18},{7,19},{8,28},{9,... | collective-permute-start | bytes 24584 | tf_op jit(solution)/shard_map/ppermute | solution.py:267
  12.6 3.1 %collective-permute-start.4 = (f32[16,128]{1,0:T(8,128)S(1)}, f32[16,128]{1,0:T(8,128)S(1)}, u32[]{:S(2)}, u32[]{:S(2)}) collective-permute-start(f32[16,128]{1,0:T(8,128)S(1)} %add.14), channel_id=1, source_target_pairs={{0,5},{1,4},{2,7},{3,6},{4,1},{5,0},{6,3},{7,2},{8,13},{9,12},{10,... | collective-permute-start | bytes 24584 | tf_op jit(solution)/shard_map/ppermute | solution.py:267
  15.7 4.0 %collective-permute-start.5 = (f32[16,128]{1,0:T(8,128)S(1)}, f32[16,128]{1,0:T(8,128)S(1)}, u32[]{:S(2)}, u32[]{:S(2)}) collective-permute-start(f32[16,128]{1,0:T(8,128)S(1)} %add.15.refs_0_), channel_id=1, source_target_pairs={{0,6},{1,7},{2,4},{3,5},{4,2},{5,3},{6,0},{7,1},{8,14},{9,15},{10,... | collective-permute-start | bytes 24584 | tf_op jit(solution)/shard_map/ppermute | solution.py:267

commit v3 on v2

--- a/solution.py
+++ b/solution.py
@@ -135,32 +135,30 @@
     nsteps = (entries - 1) // 2
     rows = tables_ref.shape[1]
     depth, first_slice = lax.axis_index("gz"), lax.axis_index("ta") * slices
-    lane = lax.broadcasted_iota(jnp.int32, (8, LANES), 1)
-    lane_slice, lane_part, lane_p = lane // 8, (lane // 4) % 2, lane % 4
-    momentum = jnp.zeros((8, LANES), jnp.int32)
-    origin = jnp.zeros((8, LANES), jnp.int32)
+    lane = lax.broadcasted_iota(jnp.int32, (rows, LANES), 1)
+    slot = lax.broadcasted_iota(jnp.int32, (rows, LANES), 0) * (LANES // 8) + lane // 8
+    lane_part, lane_p = (lane // 4) % 2, lane % 4
+    momentum = jnp.zeros((rows, LANES), jnp.int32)
     for p in range(4):
         momentum = jnp.where(lane_p == p, momenta_ref[p], momentum)
-        for t in range(slices_all):
-            origin = jnp.where((lane_p == p) & (lane_slice == t), source_ref[t, p], origin)
-    row = lax.broadcasted_iota(jnp.int32, (rows, LANES), 0)
-    for l in range(entries):
-        ahead = max(nsteps - l, 0)
-        turn = lax.rem(momentum * (depth + ahead + depth_count - origin), depth_count)
-        angle = turn.astype(f32) * (2.0 * math.pi / depth_count)
-        cosine, sine = jnp.cos(angle) * scaling, jnp.sin(angle) * scaling
-        first = jnp.where(lane_part == 0, cosine, -sine)
-        second = jnp.where(lane_part == 0, sine, cosine)
-        if l < nsteps:
-            second = -second
-        place = sum(jnp.where(entry_ref[j] == l, j, 0) for j in range(entries))
-        for now in range(slices):
-            own = lane_slice == first_slice + now
+    for now in range(slices):
+        origin = jnp.zeros((rows, LANES), jnp.int32)
+        for p in range(4):
+            origin = jnp.where(lane_p == p, source_ref[first_slice + now, p], origin)
+        for l in range(entries):
+            ahead = max(nsteps - l, 0)
+            turn = lax.rem(momentum * (depth + ahead + depth_count - origin), depth_count)
+            angle = turn.astype(f32) * (2.0 * math.pi / depth_count)
+            cosine, sine = jnp.cos(angle) * scaling, jnp.sin(angle) * scaling
+            first = jnp.where(lane_part == 0, cosine, -sine)
+            second = jnp.where(lane_part == 0, sine, cosine)
+            if l < nsteps:
+                second = -second
+            place = sum(jnp.where(entry_ref[j] == l, j, 0) for j in range(entries))
             for g in range(4):
-                hit = row == place * 4 + g
-                for which, table in ((0, first), (1, second)):
-                    mine = jnp.where(own, table, 0.0)[0:1, :]
-                    tables_ref[((now * entries + l) * 4 + g) * 2 + which] = jnp.where(hit, mine, 0.0)
+                at = ((now * entries + l) * 4 + g) * 2
+                tables_ref[at] = jnp.where(slot == place * 4 + g, first, 0.0)
+                tables_ref[at + 1] = jnp.where(slot == place * 4 + g, second, 0.0)
 
 
 def first_kernel(slices, sizes, scaling, entries, source_z_ref, entry_ref, momenta_ref, perm_ref, turn_ref, source_ref, links_ref,
@@ -222,9 +220,9 @@
 def last_kernel(slices, nsteps, left_ref, moved_ref, tables_ref, *rest):
     earlier, (out_ref, wide_ref, rows_ref) = rest[:nsteps], rest[nsteps:]
     widen(moved_ref, wide_ref)
-    total = None
     entries = 2 * nsteps + 1
     for now in range(slices):
+        total = None
         rows_ref[nsteps * 8 : nsteps * 8 + 8, :] = earlier[0][now * 8 : now * 8 + 8, :]
         for reach in range(1, nsteps):
             rows_ref[(nsteps + reach) * 8 : (nsteps + reach) * 8 + 8, :] = earlier[reach][now * 16 : now * 16 + 8, :]
@@ -239,32 +237,27 @@
                 at = ((now * entries + l) * 4 + g) * 2
                 part = rows_ref[l * 8 + g : l * 8 + g + 1, :] * tables_ref[at] + rows_ref[l * 8 + 4 + g : l * 8 + 5 + g, :] * tables_ref[at + 1]
                 total = part if total is None else total + part
-    out_ref[...] = total
-
-
-def final_kernel(slices_all, entries, mine_ref, other_ref, out_ref):
-    total = mine_ref[...] + other_ref[...]
-    for t in range(slices_all):
-        for c in range(2):
-            for row in range(entries):
-                at = t * 8 + c * 4
-                out_ref[t, row // 4, row % 4, c : c + 1, :] = total[row : row + 1, at : at + 4]
+        for row in range(tables_ref.shape[1]):
+            at = now * tables_ref.shape[1] + row
+            out_ref[:, at * LANES : (at + 1) * LANES] = jnp.broadcast_to(total[row : row + 1, :], (out_ref.shape[0], LANES))
+
+
+def final_kernel(slices, entries, width, parts_ref, out_ref):
+    peers = parts_ref.shape[0]
+    sections = out_ref.shape[0] // slices
+    each = peers // sections
+    for section in range(sections):
+        total = jnp.sum(parts_ref[section * each : (section + 1) * each, :], axis=0, keepdims=True)
+        for now in range(slices):
+            for entry in range(entries * 4):
+                for c in range(2):
+                    at = now * width + entry * 8 + c * 4
+                    out_ref[section * slices + now, entry // 4, entry % 4, c : c + 1, :] = total[:, at : at + 4]
 
 
 def from_behind(array, axis, by):
     peers = lax.axis_size(axis)
     return lax.ppermute(array, axis, [(i, (i + by) % peers) for i in range(peers)])
-
-
-def swap(array, mapping, sizes, axes):
-    nt, nz, ny = sizes
-    pairs = []
-    for t in range(nt):
-        for z in range(nz):
-            for y in range(ny):
-                a, b, c = mapping(t, z, y)
-                pairs.append(((t * nz + z) * ny + y, (a * nz + b) * ny + c))
-    return lax.ppermute(array, axes, pairs)
 
 
 def body(propagator, links, source_z, displacements, momenta, gamma_perm, gamma_phase):
@@ -282,7 +275,9 @@
     moved, moved_links = source, linked
     wide = pltpu.VMEM((288 * slices + 16 * slices, sites), f32)
     plain = pltpu.VMEM((slices * 8 * PAD, sites), f32)
-    rows = -(-entries * 4 // 8) * 8
+    rows = -(-entries * 32 // LANES)
+    width = rows * LANES
+    peers = sizes[0] * sizes[1] * sizes[2]
 
     moved = from_behind(moved, "gz", -1)
     shape_left = kept((slices * 64 * PAD, sites))
@@ -319,34 +314,20 @@
         )(gamma_perm, gamma_phase, source, moved_links, near(wilson))
     total = pl.pallas_call(
         lambda *refs: last_kernel(slices, nsteps, *refs),
-        out_shape=kept((rows, LANES)),
+        out_shape=kept((peers, slices * width)),
         in_specs=vmem(3 + nsteps),
         out_specs=vmem(1)[0],
         scratch_shapes=[wide, pltpu.VMEM((entries * 8 + 16, sites), f32)],
         name="last",
     )(near(left), near(moved), near(tables), *(near(e) for e in earlier))
 
-    moves = []
-    bit = 1
-    while bit < sizes[1]:
-        moves.append((0, bit, 0) if bit == 1 else (0, bit + 1, 0))
-        bit *= 2
-    for axis, size in ((0, sizes[0]), (2, sizes[2])):
-        bit = 1
-        while bit < size:
-            moves.append(tuple(bit if a == axis else (1 if a == 1 else 0) for a in range(3)))
-            bit *= 2
-    received = None
-    for t_bits, z_bits, y_bits in moves:
-        if received is not None:
-            total = total + received
-        received = swap(total, lambda t, z, y: (t ^ t_bits, z ^ z_bits, y ^ y_bits), sizes, axes)
+    parts = lax.all_to_all(jnp.reshape(total, (peers, 1, slices * width)), axes, 0, 0)
     out = pl.pallas_call(
-        lambda *refs: final_kernel(slices_all, entries * 4, *refs),
+        lambda *refs: final_kernel(slices, entries, width, *refs),
         out_shape=jax.ShapeDtypeStruct((slices_all, entries, 4, 2, 4), f32),
-        in_specs=vmem(2),
+        in_specs=vmem(1),
         name="final",
-    )(near(total), near(received))
+    )(near(jnp.reshape(parts, (peers, slices * width))))
     return jnp.transpose(out, (0, 1, 2, 4, 3))
 
 

time: 20.5 us -> 18.9 us (0.922)
  blocking collectives: 0 us -> 13 us
  starting transfers between devices: 9.97 us -> 2.43 us
  waiting for transfers between devices: 7.57 us -> 0.45 us
    all_to_all x0 -> x1, blocking collectives: none -> 13 us  [body(): lax.all_to_all(jnp.reshape(total, (peers, 1, slices * width)), axes, 0, 0)]
    ppermute x5 -> x0, starting transfers between devices: 7.54 us -> none  [swap(): return lax.ppermute(array, axes, pairs)]
    ppermute x5 -> x0, waiting for transfers between devices: 7.12 us -> none  [swap(): return lax.ppermute(array, axes, pairs)]
  transfers between devices with their start and end apart: 6 -> 1, of which waited for: 6 -> 1; matrix products, arithmetic and copies ran while one was open for 0% -> 0% of each run, Pallas kernels for 9% -> 10%
where the time goes in v3:
time: 18.9 us; the launch traced here: 18.8 us
  blocking collectives  13 us (69%)
  Pallas kernels  2.86 us (15%)
  starting transfers between devices  2.43 us (13%)
  waiting for transfers between devices  0.45 us (2%)
    all_to_all x1, blocking collectives, body(): lax.all_to_all(jnp.reshape(total, (peers, 1, slices * width)), axes, 0, 0)  13 us
    ppermute x1, starting transfers between devices, from_behind(): lax.ppermute(array, axis, [(i, (i + by) % peers) for i in range(peers)])  2.43 us
    pallas_call x1, Pallas kernels, body(): pl.pallas_call(lambda *refs: first_kernel(slices, (slices_all, depth_coun...  1.84 us
    pallas_call x1, Pallas kernels, body(): pl.pallas_call(lambda *refs: final_kernel(slices, entries, width, *refs),...  0.73 us
    ppermute x1, waiting for transfers between devices, from_behind(): lax.ppermute(array, axis, [(i, (i + by) % peers) for i in range(peers)])  0.45 us
  transfers between devices with their start and end apart: 1, of which 1 were waited for; matrix products, arithmetic and copies ran while one was open for 0% of the time, Pallas kernels for 10%

profile of v3, /device:TPU:0, one launch (start us, length us, event | category | flops | bytes accessed | tf_op | source)
XLA Modules:
  0.0 18.8 jit_solution(13237795497689939566)
XLA Ops:
  0.0 2.4 %collective-permute-start = (bf16[288,128]{1,0:T(8,128)(2,1)}, bf16[288,128]{1,0:T(8,128)(2,1)S(1)}, u32[]{:S(2)}, u32[]{:S(2)}) collective-permute-start(bf16[288,128]{1,0:T(8,128)(2,1)} %bitcast.15), channel_id=1, source_target_pairs={{0,12},{4,0},{8,4},{12,8},{1,13},{5,1},{9,5},{13,9},{2,14},{6,2},{... | collective-permute-start | bytes 221192 | tf_op jit(solution)/shard_map/ppermute | solution.py:260
  2.4 1.8 %local.1 = (f32[2560,128]{1,0:T(8,128)S(1)}, f32[8,128]{1,0:T(8,128)S(1)}, f32[24,1,128]{2,1,0:T(1,128)S(1)}, f32[18,128]{1,0:T(8,128)}) custom-call(s32[2,4]{1,0:T(2,128)} %refs_0_.1, s32[3]{0:T(128)} %refs_1_.1, s32[4]{0:T(128)} %refs_2_.1, s32[4,4]{1,0:T(4,128)} %refs_3_.1, s32[4,4]{1,0:T(4,128)} %refs_4_.1, bf16[288,128]{1,0:T(8,128)(2,1)} %bitcast.16, ...), custom_call_target="tpu_custom_call" | custom-call | tf_op jit(solution)/shard_map/local/pallas_call | solution.py:285
  4.3 0.5 %collective-permute-done.refs_1_ = bf16[288,128]{1,0:T(8,128)(2,1)S(1)} collective-permute-done((bf16[288,128]{1,0:T(8,128)(2,1)}, bf16[288,128]{1,0:T(8,128)(2,1)S(1)}, u32[]{:S(2)}, u32[]{:S(2)}) %collective-permute-start) | collective-permute-done | bytes 73760 | tf_op jit(solution)/shard_map/ppermute | solution.py:260
  4.7 0.3 %last.1 = f32[32,128]{1,0:T(8,128)S(1)} custom-call(f32[2560,128]{1,0:T(8,128)S(1)} %get-tuple-element.8.refs_0_, bf16[288,128]{1,0:T(8,128)(2,1)S(1)} %collective-permute-done.refs_1_, f32[24,1,128]{2,1,0:T(1,128)S(1)} %get-tuple-element.9.refs_2_, f32[8,128]{1,0:T(8,128)S(1)} %get-tuple-element.10.refs_3_), custom_call_target="tpu_custom_call" | custom-call | tf_op jit(solution)/shard_map/last/pallas_call | solution.py:315
  5.0 13.0 %all_to_all.5 = f32[32,1,128]{2,1,0:T(1,128)S(1)} all-to-all(f32[32,1,128]{2,1,0:T(1,128)S(1)} %bitcast.13), channel_id=1, replica_groups=mesh['ta'=2,'gz'=4,'gy'=4] {'ta','gz','gy'}, dimensions={0} | all-to-all | bytes 32768 | tf_op jit(solution)/shard_map/all_to_all | solution.py:324
  18.0 0.7 %final.1 = f32[2,3,4,2,4]{4,3,2,1,0:T(2,128)} custom-call(f32[32,128]{1,0:T(8,128)S(1)} %bitcast.14), custom_call_target="tpu_custom_call" | custom-call | tf_op jit(solution)/shard_map/final/pallas_call | solution.py:325
Async XLA Ops:
  0.0 4.7 %collective-permute-start = (bf16[288,128]{1,0:T(8,128)(2,1)}, bf16[288,128]{1,0:T(8,128)(2,1)S(1)}, u32[]{:S(2)}, u32[]{:S(2)}) collective-permute-start(bf16[288,128]{1,0:T(8,128)(2,1)} %bitcast.15), channel_id=1, source_target_pairs={{0,12},{4,0},{8,4},{12,8},{1,13},{5,1},{9,5},{13,9},{2,14},{6,2},{... | collective-permute-start | bytes 221192 | tf_op jit(solution)/shard_map/ppermute | solution.py:260

commit v4 on v3

--- a/solution.py
+++ b/solution.py
@@ -239,20 +239,26 @@
                 total = part if total is None else total + part
         for row in range(tables_ref.shape[1]):
             at = now * tables_ref.shape[1] + row
-            out_ref[:, at * LANES : (at + 1) * LANES] = jnp.broadcast_to(total[row : row + 1, :], (out_ref.shape[0], LANES))
-
-
-def final_kernel(slices, entries, width, parts_ref, out_ref):
-    peers = parts_ref.shape[0]
-    sections = out_ref.shape[0] // slices
-    each = peers // sections
-    for section in range(sections):
-        total = jnp.sum(parts_ref[section * each : (section + 1) * each, :], axis=0, keepdims=True)
+            out_ref[:, at * LANES : (at + 1) * LANES] = total[row : row + 1, :]
+
+
+def final_kernel(slices, entries, width, owners, parts_ref, out_ref):
+    for section in range(out_ref.shape[0] // slices):
+        total = sum(parts_ref[i : i + 1, :] for i, owner in enumerate(owners) if owner == section)
         for now in range(slices):
             for entry in range(entries * 4):
                 for c in range(2):
                     at = now * width + entry * 8 + c * 4
                     out_ref[section * slices + now, entry // 4, entry % 4, c : c + 1, :] = total[:, at : at + 4]
+
+
+def chips_and_groups(sizes):
+    nt, nz, ny = sizes
+    chips = [(t, b, y) for t in range(nt) for b in range(nz // 2) for y in range(ny)]
+    corner = chips[-1]
+    chips.sort(key=lambda chip: (sum(abs(i - j) for i, j in zip(chip, corner)), chip))
+    groups = [[(t * nz + 2 * b + (half + t + b + y) % 2) * ny + y for t, b, y in chips] for half in range(2)]
+    return chips, groups
 
 
 def from_behind(array, axis, by):
@@ -277,7 +283,6 @@
     plain = pltpu.VMEM((slices * 8 * PAD, sites), f32)
     rows = -(-entries * 32 // LANES)
     width = rows * LANES
-    peers = sizes[0] * sizes[1] * sizes[2]
 
     moved = from_behind(moved, "gz", -1)
     shape_left = kept((slices * 64 * PAD, sites))
@@ -314,20 +319,23 @@
         )(gamma_perm, gamma_phase, source, moved_links, near(wilson))
     total = pl.pallas_call(
         lambda *refs: last_kernel(slices, nsteps, *refs),
-        out_shape=kept((peers, slices * width)),
+        out_shape=kept((1, slices * width)),
         in_specs=vmem(3 + nsteps),
         out_specs=vmem(1)[0],
         scratch_shapes=[wide, pltpu.VMEM((entries * 8 + 16, sites), f32)],
         name="last",
     )(near(left), near(moved), near(tables), *(near(e) for e in earlier))
 
-    parts = lax.all_to_all(jnp.reshape(total, (peers, 1, slices * width)), axes, 0, 0)
+    total = total + lax.ppermute(total, "gz", [(i, i ^ 1) for i in range(sizes[1])])
+    chips, groups = chips_and_groups(sizes)
+    copies = jnp.broadcast_to(total[None], (len(chips), 1, slices * width))
+    parts = lax.all_to_all(copies, axes, 0, 0, axis_index_groups=groups)
     out = pl.pallas_call(
-        lambda *refs: final_kernel(slices, entries, width, *refs),
+        lambda *refs: final_kernel(slices, entries, width, [chip[0] for chip in chips], *refs),
         out_shape=jax.ShapeDtypeStruct((slices_all, entries, 4, 2, 4), f32),
         in_specs=vmem(1),
         name="final",
-    )(near(jnp.reshape(parts, (peers, slices * width))))
+    )(near(jnp.reshape(parts, (len(chips), slices * width))))
     return jnp.transpose(out, (0, 1, 2, 4, 3))
 
 

time: 18.9 us -> 17.6 us (0.931)
  blocking collectives: 13 us -> 10.2 us
  waiting for transfers between devices: 0.45 us -> 1.27 us
  starting transfers between devices: 2.43 us -> 3.06 us
    all_to_all x1, blocking collectives: 13 us -> 10.2 us  [body(): parts = lax.all_to_all(copies, axes, 0, 0, axis_index_groups=groups)]
    ppermute x0 -> x1, waiting for transfers between devices: none -> 0.82 us  [body(): lax.ppermute(total, 'gz', [(i, i ^ 1) for i in range(sizes[1])])]
    ppermute x0 -> x1, starting transfers between devices: none -> 0.62 us  [body(): lax.ppermute(total, 'gz', [(i, i ^ 1) for i in range(sizes[1])])]
  transfers between devices with their start and end apart: 1 -> 2, of which waited for: 1 -> 2; matrix products, arithmetic and copies ran while one was open for 0% -> 0% of each run, Pallas kernels for 10% -> 11%
where the time goes in v4:
time: 17.6 us; the launch traced here: 17.4 us
  blocking collectives  10.2 us (58%)
  starting transfers between devices  3.06 us (17%)
  Pallas kernels  2.86 us (16%)
  waiting for transfers between devices  1.27 us (7%)
    all_to_all x1, blocking collectives, body(): parts = lax.all_to_all(copies, axes, 0, 0, axis_index_groups=groups)  10.2 us
    ppermute x1, starting transfers between devices, from_behind(): lax.ppermute(array, axis, [(i, (i + by) % peers) for i in range(peers)])  2.43 us
    pallas_call x1, Pallas kernels, body(): pl.pallas_call(lambda *refs: first_kernel(slices, (slices_all, depth_coun...  1.84 us
    ppermute x1, waiting for transfers between devices, body(): lax.ppermute(total, 'gz', [(i, i ^ 1) for i in range(sizes[1])])  0.82 us
    pallas_call x1, Pallas kernels, body(): pl.pallas_call(lambda *refs: final_kernel(slices, entries, width, [chip[0...  0.73 us
    ppermute x1, starting transfers between devices, body(): lax.ppermute(total, 'gz', [(i, i ^ 1) for i in range(sizes[1])])  0.62 us
    ppermute x1, waiting for transfers between devices, from_behind(): lax.ppermute(array, axis, [(i, (i + by) % peers) for i in range(peers)])  0.45 us
  transfers between devices with their start and end apart: 2, of which 2 were waited for; matrix products, arithmetic and copies ran while one was open for 0% of the time, Pallas kernels for 11%

profile of v4, /device:TPU:0, one launch (start us, length us, event | category | flops | bytes accessed | tf_op | source)
XLA Modules:
  0.0 17.4 jit_solution(2476069024017560588)
XLA Ops:
  0.0 2.4 %collective-permute-start = (bf16[288,128]{1,0:T(8,128)(2,1)}, bf16[288,128]{1,0:T(8,128)(2,1)S(1)}, u32[]{:S(2)}, u32[]{:S(2)}) collective-permute-start(bf16[288,128]{1,0:T(8,128)(2,1)} %bitcast.13), channel_id=1, source_target_pairs={{0,12},{4,0},{8,4},{12,8},{1,13},{5,1},{9,5},{13,9},{2,14},{6,2},{... | collective-permute-start | bytes 221192 | tf_op jit(solution)/shard_map/ppermute | solution.py:266
  2.4 1.8 %local.1 = (f32[2560,128]{1,0:T(8,128)S(1)}, f32[8,128]{1,0:T(8,128)S(1)}, f32[24,1,128]{2,1,0:T(1,128)S(1)}, f32[18,128]{1,0:T(8,128)}) custom-call(s32[2,4]{1,0:T(2,128)} %refs_0_.1, s32[3]{0:T(128)} %refs_1_.1, s32[4]{0:T(128)} %refs_2_.1, s32[4,4]{1,0:T(4,128)} %refs_3_.1, s32[4,4]{1,0:T(4,128)} %refs_4_.1, bf16[288,128]{1,0:T(8,128)(2,1)} %bitcast.14, ...), custom_call_target="tpu_custom_call" | custom-call | tf_op jit(solution)/shard_map/local/pallas_call | solution.py:290
  4.3 0.5 %collective-permute-done.refs_1_ = bf16[288,128]{1,0:T(8,128)(2,1)S(1)} collective-permute-done((bf16[288,128]{1,0:T(8,128)(2,1)}, bf16[288,128]{1,0:T(8,128)(2,1)S(1)}, u32[]{:S(2)}, u32[]{:S(2)}) %collective-permute-start) | collective-permute-done | bytes 73760 | tf_op jit(solution)/shard_map/ppermute | solution.py:266
  4.7 0.3 %last.1 = f32[1,128]{1,0:T(1,128)S(1)} custom-call(f32[2560,128]{1,0:T(8,128)S(1)} %get-tuple-element.8.refs_0_, bf16[288,128]{1,0:T(8,128)(2,1)S(1)} %collective-permute-done.refs_1_, f32[24,1,128]{2,1,0:T(1,128)S(1)} %get-tuple-element.9.refs_2_, f32[8,128]{1,0:T(8,128)S(1)} %get-tuple-element.10.refs_3_), custom_call_target="tpu_custom_call" | custom-call | tf_op jit(solution)/shard_map/last/pallas_call | solution.py:320
  5.0 0.6 %collective-permute-start.1 = (f32[1,128]{1,0:T(1,128)S(1)}, f32[1,128]{1,0:T(1,128)S(1)}, u32[]{:S(2)}, u32[]{:S(2)}) collective-permute-start(f32[1,128]{1,0:T(1,128)S(1)} %last.1), channel_id=1, source_target_pairs={{0,4},{4,0},{8,12},{12,8},{1,5},{5,1},{9,13},{13,9},{2,6},{6,2},{1... | collective-permute-start | bytes 1544 | tf_op jit(solution)/shard_map/ppermute | solution.py:329
  5.6 0.8 %collective-permute-done.1 = f32[1,128]{1,0:T(1,128)S(1)} collective-permute-done((f32[1,128]{1,0:T(1,128)S(1)}, f32[1,128]{1,0:T(1,128)S(1)}, u32[]{:S(2)}, u32[]{:S(2)}) %collective-permute-start.1) | collective-permute-done | bytes 544 | tf_op jit(solution)/shard_map/ppermute | solution.py:329
  6.5 10.2 %all_to_all.5 = f32[16,1,128]{2,1,0:T(1,128)S(1)} all-to-all(f32[16,1,128]{2,1,0:T(1,128)S(1)} %broadcast_in_dim.9), channel_id=1, replica_groups={{31,11,19,26,7,14,22,29,2,9,17,24,5,12,20,0},{27,15,23,30,3,10,18,25,6,..., dimensions={0} | all-to-all | bytes 16384 | tf_op jit(solution)/shard_map/all_to_all | solution.py:332
  16.6 0.7 %final.1 = f32[2,3,4,2,4]{4,3,2,1,0:T(2,128)} custom-call(f32[16,128]{1,0:T(8,128)S(1)} %bitcast.12), custom_call_target="tpu_custom_call" | custom-call | tf_op jit(solution)/shard_map/final/pallas_call | solution.py:333
  (2 shorter events, 0.0 us)
Async XLA Ops:
  0.0 4.7 %collective-permute-start = (bf16[288,128]{1,0:T(8,128)(2,1)}, bf16[288,128]{1,0:T(8,128)(2,1)S(1)}, u32[]{:S(2)}, u32[]{:S(2)}) collective-permute-start(bf16[288,128]{1,0:T(8,128)(2,1)} %bitcast.13), channel_id=1, source_target_pairs={{0,12},{4,0},{8,4},{12,8},{1,13},{5,1},{9,5},{13,9},{2,14},{6,2},{... | collective-permute-start | bytes 221192 | tf_op jit(solution)/shard_map/ppermute | solution.py:266
  5.0 1.4 %collective-permute-start.1 = (f32[1,128]{1,0:T(1,128)S(1)}, f32[1,128]{1,0:T(1,128)S(1)}, u32[]{:S(2)}, u32[]{:S(2)}) collective-permute-start(f32[1,128]{1,0:T(1,128)S(1)} %last.1), channel_id=1, source_target_pairs={{0,4},{4,0},{8,12},{12,8},{1,5},{5,1},{9,13},{13,9},{2,6},{6,2},{1... | collective-permute-start | bytes 1544 | tf_op jit(solution)/shard_map/ppermute | solution.py:329

commit v5 on v4

--- a/solution.py
+++ b/solution.py
@@ -242,9 +242,9 @@
             out_ref[:, at * LANES : (at + 1) * LANES] = total[row : row + 1, :]
 
 
-def final_kernel(slices, entries, width, owners, parts_ref, out_ref):
+def final_kernel(slices, entries, width, owners, mine_ref, other_ref, out_ref):
     for section in range(out_ref.shape[0] // slices):
-        total = sum(parts_ref[i : i + 1, :] for i, owner in enumerate(owners) if owner == section)
+        total = sum(ref[i : i + 1, :] for ref in (mine_ref, other_ref) for i, owner in enumerate(owners) if owner == section)
         for now in range(slices):
             for entry in range(entries * 4):
                 for c in range(2):
@@ -257,7 +257,7 @@
     chips = [(t, b, y) for t in range(nt) for b in range(nz // 2) for y in range(ny)]
     corner = chips[-1]
     chips.sort(key=lambda chip: (sum(abs(i - j) for i, j in zip(chip, corner)), chip))
-    groups = [[(t * nz + 2 * b + (half + t + b + y) % 2) * ny + y for t, b, y in chips] for half in range(2)]
+    groups = [[(t * nz + 2 * b + half) * ny + y for t, b, y in chips] for half in range(2)]
     return chips, groups
 
 
@@ -326,16 +326,17 @@
         name="last",
     )(near(left), near(moved), near(tables), *(near(e) for e in earlier))
 
-    total = total + lax.ppermute(total, "gz", [(i, i ^ 1) for i in range(sizes[1])])
     chips, groups = chips_and_groups(sizes)
     copies = jnp.broadcast_to(total[None], (len(chips), 1, slices * width))
     parts = lax.all_to_all(copies, axes, 0, 0, axis_index_groups=groups)
+    mine = jnp.reshape(parts, (len(chips), slices * width))
+    other = lax.ppermute(mine, "gz", [(i, i ^ 1) for i in range(sizes[1])])
     out = pl.pallas_call(
         lambda *refs: final_kernel(slices, entries, width, [chip[0] for chip in chips], *refs),
         out_shape=jax.ShapeDtypeStruct((slices_all, entries, 4, 2, 4), f32),
-        in_specs=vmem(1),
+        in_specs=vmem(2),
         name="final",
-    )(near(jnp.reshape(parts, (len(chips), slices * width))))
+    )(near(mine), near(other))
     return jnp.transpose(out, (0, 1, 2, 4, 3))
 
 

time: 17.6 us -> 16.6 us (0.943)
  blocking collectives: 10.2 us -> 9.46 us
  starting transfers between devices: 3.06 us -> 2.69 us
    all_to_all x1, blocking collectives: 10.2 us -> 9.46 us  [body(): parts = lax.all_to_all(copies, axes, 0, 0, axis_index_groups=groups)]
    ppermute x1, starting transfers between devices: 0.62 us -> 0.25 us  [body(): other = lax.ppermute(mine, 'gz', [(i, i ^ 1) for i in range(sizes[1])])]
where the time goes in v5:
time: 16.6 us; the launch traced here: 16.4 us
  blocking collectives  9.46 us (57%)
  Pallas kernels  2.87 us (17%)
  starting transfers between devices  2.69 us (16%)
  waiting for transfers between devices  1.37 us (8%)
    all_to_all x1, blocking collectives, body(): parts = lax.all_to_all(copies, axes, 0, 0, axis_index_groups=groups)  9.46 us
    ppermute x1, starting transfers between devices, from_behind(): lax.ppermute(array, axis, [(i, (i + by) % peers) for i in range(peers)])  2.43 us
    pallas_call x1, Pallas kernels, body(): pl.pallas_call(lambda *refs: first_kernel(slices, (slices_all, depth_coun...  1.84 us
    ppermute x1, waiting for transfers between devices, body(): other = lax.ppermute(mine, 'gz', [(i, i ^ 1) for i in range(sizes[1])])  0.92 us
    pallas_call x1, Pallas kernels, body(): pl.pallas_call(lambda *refs: final_kernel(slices, entries, width, [chip[0...  0.74 us
    ppermute x1, waiting for transfers between devices, from_behind(): lax.ppermute(array, axis, [(i, (i + by) % peers) for i in range(peers)])  0.45 us
  transfers between devices with their start and end apart: 2, of which 2 were waited for; matrix products, arithmetic and copies ran while one was open for 0% of the time, Pallas kernels for 11%

profile of v5, /device:TPU:0, one launch (start us, length us, event | category | flops | bytes accessed | tf_op | source)
XLA Modules:
  0.0 16.4 jit_solution(564064703186847713)
XLA Ops:
  0.0 2.4 %collective-permute-start = (bf16[288,128]{1,0:T(8,128)(2,1)}, bf16[288,128]{1,0:T(8,128)(2,1)S(1)}, u32[]{:S(2)}, u32[]{:S(2)}) collective-permute-start(bf16[288,128]{1,0:T(8,128)(2,1)} %bitcast.14), channel_id=1, source_target_pairs={{0,12},{4,0},{8,4},{12,8},{1,13},{5,1},{9,5},{13,9},{2,14},{6,2},{... | collective-permute-start | bytes 221192 | tf_op jit(solution)/shard_map/ppermute | solution.py:266
  2.4 1.8 %local.1 = (f32[2560,128]{1,0:T(8,128)S(1)}, f32[8,128]{1,0:T(8,128)S(1)}, f32[24,1,128]{2,1,0:T(1,128)S(1)}, f32[18,128]{1,0:T(8,128)}) custom-call(s32[2,4]{1,0:T(2,128)} %refs_0_.1, s32[3]{0:T(128)} %refs_1_.1, s32[4]{0:T(128)} %refs_2_.1, s32[4,4]{1,0:T(4,128)} %refs_3_.1, s32[4,4]{1,0:T(4,128)} %refs_4_.1, bf16[288,128]{1,0:T(8,128)(2,1)} %bitcast.15, ...), custom_call_target="tpu_custom_call" | custom-call | tf_op jit(solution)/shard_map/local/pallas_call | solution.py:290
  4.3 0.5 %collective-permute-done.refs_1_ = bf16[288,128]{1,0:T(8,128)(2,1)S(1)} collective-permute-done((bf16[288,128]{1,0:T(8,128)(2,1)}, bf16[288,128]{1,0:T(8,128)(2,1)S(1)}, u32[]{:S(2)}, u32[]{:S(2)}) %collective-permute-start) | collective-permute-done | bytes 73760 | tf_op jit(solution)/shard_map/ppermute | solution.py:266
  4.7 0.3 %last.1 = f32[1,128]{1,0:T(1,128)S(1)} custom-call(f32[2560,128]{1,0:T(8,128)S(1)} %get-tuple-element.8.refs_0_, bf16[288,128]{1,0:T(8,128)(2,1)S(1)} %collective-permute-done.refs_1_, f32[24,1,128]{2,1,0:T(1,128)S(1)} %get-tuple-element.9.refs_2_, f32[8,128]{1,0:T(8,128)S(1)} %get-tuple-element.10.refs_3_), custom_call_target="tpu_custom_call" | custom-call | tf_op jit(solution)/shard_map/last/pallas_call | solution.py:320
  5.0 9.5 %all_to_all.5 = f32[16,1,128]{2,1,0:T(1,128)S(1)} all-to-all(f32[16,1,128]{2,1,0:T(1,128)S(1)} %broadcast_in_dim.9), channel_id=1, replica_groups={{27,11,19,26,3,10,18,25,2,9,17,24,1,8,16,0},{31,15,23,30,7,14,22,29,6,1..., dimensions={0} | all-to-all | bytes 16384 | tf_op jit(solution)/shard_map/all_to_all | solution.py:331
  14.5 0.3 %collective-permute-start.1 = (f32[16,128]{1,0:T(8,128)S(1)}, f32[16,128]{1,0:T(8,128)S(1)}, u32[]{:S(2)}, u32[]{:S(2)}) collective-permute-start(f32[16,128]{1,0:T(8,128)S(1)} %bitcast.11), channel_id=1, source_target_pairs={{0,4},{4,0},{8,12},{12,8},{1,5},{5,1},{9,13},{13,9},{2,6},{6,2},{1... | collective-permute-start | bytes 24584 | tf_op jit(solution)/shard_map/ppermute | solution.py:333
  14.8 0.9 %collective-permute-done.1.refs_1_ = f32[16,128]{1,0:T(8,128)S(1)} collective-permute-done((f32[16,128]{1,0:T(8,128)S(1)}, f32[16,128]{1,0:T(8,128)S(1)}, u32[]{:S(2)}, u32[]{:S(2)}) %collective-permute-start.1) | collective-permute-done | bytes 8224 | tf_op jit(solution)/shard_map/ppermute | solution.py:333
  15.7 0.7 %final.1 = f32[2,3,4,2,4]{4,3,2,1,0:T(2,128)} custom-call(f32[16,128]{1,0:T(8,128)S(1)} %bitcast.12, f32[16,128]{1,0:T(8,128)S(1)} %collective-permute-done.1.refs_1_), custom_call_target="tpu_custom_call" | custom-call | tf_op jit(solution)/shard_map/final/pallas_call | solution.py:334
  (1 shorter events, 0.0 us)
Async XLA Ops:
  0.0 4.7 %collective-permute-start = (bf16[288,128]{1,0:T(8,128)(2,1)}, bf16[288,128]{1,0:T(8,128)(2,1)S(1)}, u32[]{:S(2)}, u32[]{:S(2)}) collective-permute-start(bf16[288,128]{1,0:T(8,128)(2,1)} %bitcast.14), channel_id=1, source_target_pairs={{0,12},{4,0},{8,4},{12,8},{1,13},{5,1},{9,5},{13,9},{2,14},{6,2},{... | collective-permute-start | bytes 221192 | tf_op jit(solution)/shard_map/ppermute | solution.py:266
  14.5 1.2 %collective-permute-start.1 = (f32[16,128]{1,0:T(8,128)S(1)}, f32[16,128]{1,0:T(8,128)S(1)}, u32[]{:S(2)}, u32[]{:S(2)}) collective-permute-start(f32[16,128]{1,0:T(8,128)S(1)} %bitcast.11), channel_id=1, source_target_pairs={{0,4},{4,0},{8,12},{12,8},{1,5},{5,1},{9,13},{13,9},{2,6},{6,2},{1... | collective-permute-start | bytes 24584 | tf_op jit(solution)/shard_map/ppermute | solution.py:333

commit v6 on v5

--- a/solution.py
+++ b/solution.py
@@ -111,6 +111,17 @@
                     left_ref[tile_at((base * 4 + 4 + put) * PAD + 8 * j), :] = cr * li + (sign * ci) * lr
 
 
+def fold(tiles):
+    row = lax.broadcasted_iota(jnp.int32, tiles[0].shape, 0)
+    for bit in (4, 2, 1):
+        half = len(tiles) // 2
+        low = row & bit == 0
+        tiles = [
+            jnp.where(low, a + pltpu.roll(a, 8 - bit, 0), b + pltpu.roll(b, bit, 0)) for a, b in zip(tiles[:half], tiles[half:])
+        ]
+    return tiles[0]
+
+
 def meet(left_ref, wide_ref, slices, now, rows_ref, first):
     sums = [None] * 16
     for u in range(4):
@@ -126,23 +137,25 @@
                 at = (which // 4) * 8 + which % 4
                 sums[at] = re if sums[at] is None else sums[at] + re
                 sums[at + 4] = im if sums[at + 4] is None else sums[at + 4] + im
-    for at in range(16):
-        rows_ref[pl.ds(first + at, 1), :] = jnp.sum(sums[at], axis=0, keepdims=True)
+    rows_ref[first : first + 8, :] = fold(sums[:8])
+    rows_ref[first + 8 : first + 16, :] = fold(sums[8:])
 
 
 def fill_tables(tables_ref, sizes, scaling, slices, entries, source_ref, entry_ref, momenta_ref):
-    slices_all, depth_count = sizes
+    _, depth_count = sizes
     nsteps = (entries - 1) // 2
-    rows = tables_ref.shape[1]
+    rows = tables_ref.shape[1] // LANES
     depth, first_slice = lax.axis_index("gz"), lax.axis_index("ta") * slices
-    lane = lax.broadcasted_iota(jnp.int32, (rows, LANES), 1)
-    slot = lax.broadcasted_iota(jnp.int32, (rows, LANES), 0) * (LANES // 8) + lane // 8
-    lane_part, lane_p = (lane // 4) % 2, lane % 4
-    momentum = jnp.zeros((rows, LANES), jnp.int32)
+    lane = lax.broadcasted_iota(jnp.int32, (8, LANES), 1)
+    sub = lax.broadcasted_iota(jnp.int32, (8, LANES), 0)
+    turned = 31 - lane // 4
+    to_imag, lane_p = turned % 2 == 1, lane % 4
+    from_imag, insertion = sub >= 4, sub % 4
+    momentum = jnp.zeros((8, LANES), jnp.int32)
     for p in range(4):
         momentum = jnp.where(lane_p == p, momenta_ref[p], momentum)
     for now in range(slices):
-        origin = jnp.zeros((rows, LANES), jnp.int32)
+        origin = jnp.zeros((8, LANES), jnp.int32)
         for p in range(4):
             origin = jnp.where(lane_p == p, source_ref[first_slice + now, p], origin)
         for l in range(entries):
@@ -150,15 +163,13 @@
             turn = lax.rem(momentum * (depth + ahead + depth_count - origin), depth_count)
             angle = turn.astype(f32) * (2.0 * math.pi / depth_count)
             cosine, sine = jnp.cos(angle) * scaling, jnp.sin(angle) * scaling
-            first = jnp.where(lane_part == 0, cosine, -sine)
-            second = jnp.where(lane_part == 0, sine, cosine)
-            if l < nsteps:
-                second = -second
+            first = jnp.where(to_imag, -sine, cosine)
+            second = jnp.where(to_imag, cosine, sine)
+            weight = jnp.where(from_imag, -second if l < nsteps else second, first)
             place = sum(jnp.where(entry_ref[j] == l, j, 0) for j in range(entries))
-            for g in range(4):
-                at = ((now * entries + l) * 4 + g) * 2
-                tables_ref[at] = jnp.where(slot == place * 4 + g, first, 0.0)
-                tables_ref[at + 1] = jnp.where(slot == place * 4 + g, second, 0.0)
+            for row in range(rows):
+                hit = row * 16 + turned // 2 == place * 4 + insertion
+                tables_ref[(now * entries + l) * 8 : (now * entries + l) * 8 + 8, row * LANES : (row + 1) * LANES] = jnp.where(hit, weight, 0.0)
 
 
 def first_kernel(slices, sizes, scaling, entries, source_z_ref, entry_ref, momenta_ref, perm_ref, turn_ref, source_ref, links_ref,
@@ -221,42 +232,46 @@
     earlier, (out_ref, wide_ref, rows_ref) = rest[:nsteps], rest[nsteps:]
     widen(moved_ref, wide_ref)
     entries = 2 * nsteps + 1
-    for now in range(slices):
+    width = tables_ref.shape[1]
+    for now in range(slices):
+        meet(left_ref, wide_ref, slices, now, rows_ref, 0)
         total = None
-        rows_ref[nsteps * 8 : nsteps * 8 + 8, :] = earlier[0][now * 8 : now * 8 + 8, :]
-        for reach in range(1, nsteps):
-            rows_ref[(nsteps + reach) * 8 : (nsteps + reach) * 8 + 8, :] = earlier[reach][now * 16 : now * 16 + 8, :]
-            rows_ref[(nsteps - reach) * 8 : (nsteps - reach) * 8 + 8, :] = earlier[reach][now * 16 + 8 : now * 16 + 16, :]
-        meet(left_ref, wide_ref, slices, now, rows_ref, entries * 8)
-        rows_ref[2 * nsteps * 8 : entries * 8, :] = rows_ref[entries * 8 : entries * 8 + 8, :]
-        rows_ref[0:8, :] = rows_ref[entries * 8 + 8 : entries * 8 + 16, :]
-        summed = jnp.sum(rows_ref[0 : entries * 8, :], axis=1, keepdims=True)
-        rows_ref[0 : entries * 8, :] = jnp.broadcast_to(summed, (entries * 8, LANES))
         for l in range(entries):
-            for g in range(4):
-                at = ((now * entries + l) * 4 + g) * 2
-                part = rows_ref[l * 8 + g : l * 8 + g + 1, :] * tables_ref[at] + rows_ref[l * 8 + 4 + g : l * 8 + 5 + g, :] * tables_ref[at + 1]
-                total = part if total is None else total + part
-        for row in range(tables_ref.shape[1]):
-            at = now * tables_ref.shape[1] + row
-            out_ref[:, at * LANES : (at + 1) * LANES] = total[row : row + 1, :]
-
-
-def final_kernel(slices, entries, width, owners, mine_ref, other_ref, out_ref):
-    for section in range(out_ref.shape[0] // slices):
-        total = sum(ref[i : i + 1, :] for ref in (mine_ref, other_ref) for i, owner in enumerate(owners) if owner == section)
+            reach = abs(l - nsteps)
+            if reach == nsteps:
+                rows = rows_ref[0:8, :] if l else rows_ref[8:16, :]
+            elif reach:
+                at = now * 16 + (0 if l > nsteps else 8)
+                rows = earlier[reach][at : at + 8, :]
+            else:
+                rows = earlier[0][now * 8 : now * 8 + 8, :]
+            summed = jnp.sum(rows, axis=1, keepdims=True)
+            part = summed * tables_ref[(now * entries + l) * 8 : (now * entries + l) * 8 + 8, :]
+            total = part if total is None else total + part
+        out_ref[:, now * width : (now + 1) * width] = jnp.sum(total, axis=0, keepdims=True)
+
+
+def final_kernel(slices, rows, owners, mine_ref, other_ref, out_ref):
+    sections = out_ref.shape[0] // (slices * rows)
+    each = len(owners) // sections
+    width = mine_ref.shape[1] // slices
+    for place in range(sections):
+        picked = slice(place * each, (place + 1) * each)
+        total = jnp.sum(mine_ref[picked, :] + other_ref[picked, :], axis=0, keepdims=True)
         for now in range(slices):
-            for entry in range(entries * 4):
-                for c in range(2):
-                    at = now * width + entry * 8 + c * 4
-                    out_ref[section * slices + now, entry // 4, entry % 4, c : c + 1, :] = total[:, at : at + 4]
+            for block in range(rows // 8):
+                at = now * width + block // 4 * LANES
+                tile = jnp.broadcast_to(total[:, at : at + LANES], (8, LANES))
+                tile = pltpu.roll(tile, 4 + 32 * (block % 4), 1, stride=4, stride_axis=0)
+                first = (owners[place * each] * slices + now) * rows + block * 8
+                out_ref[first : first + 8, :] = tile[:, 0:4]
 
 
 def chips_and_groups(sizes):
     nt, nz, ny = sizes
     chips = [(t, b, y) for t in range(nt) for b in range(nz // 2) for y in range(ny)]
     corner = chips[-1]
-    chips.sort(key=lambda chip: (sum(abs(i - j) for i, j in zip(chip, corner)), chip))
+    chips.sort(key=lambda chip: (-chip[0], sum(abs(i - j) for i, j in zip(chip, corner)), chip))
     groups = [[(t * nz + 2 * b + half) * ny + y for t, b, y in chips] for half in range(2)]
     return chips, groups
 
@@ -289,7 +304,7 @@
     shape_wilson = kept((slices * 18, sites))
     left, first_rows, tables, wilson = pl.pallas_call(
         lambda *refs: first_kernel(slices, (slices_all, depth_count), scaling, entries, *refs),
-        out_shape=(shape_left, kept((slices * 8, sites)), kept((slices * entries * 8, rows, LANES)), shape_wilson),
+        out_shape=(shape_left, kept((slices * 8, sites)), kept((slices * entries * 8, width)), shape_wilson),
         in_specs=smem(5) + vmem(2),
         out_specs=tuple(vmem(4)),
         scratch_shapes=[wide, plain, pltpu.VMEM((256, sites), f32)],
@@ -322,7 +337,7 @@
         out_shape=kept((1, slices * width)),
         in_specs=vmem(3 + nsteps),
         out_specs=vmem(1)[0],
-        scratch_shapes=[wide, pltpu.VMEM((entries * 8 + 16, sites), f32)],
+        scratch_shapes=[wide, pltpu.VMEM((16, sites), f32)],
         name="last",
     )(near(left), near(moved), near(tables), *(near(e) for e in earlier))
 
@@ -331,13 +346,14 @@
     parts = lax.all_to_all(copies, axes, 0, 0, axis_index_groups=groups)
     mine = jnp.reshape(parts, (len(chips), slices * width))
     other = lax.ppermute(mine, "gz", [(i, i ^ 1) for i in range(sizes[1])])
+    results = entries * 8
     out = pl.pallas_call(
-        lambda *refs: final_kernel(slices, entries, width, [chip[0] for chip in chips], *refs),
-        out_shape=jax.ShapeDtypeStruct((slices_all, entries, 4, 2, 4), f32),
+        lambda *refs: final_kernel(slices, results, [chip[0] for chip in chips], *refs),
+        out_shape=jax.ShapeDtypeStruct((slices_all * results, 4), f32),
         in_specs=vmem(2),
         name="final",
     )(near(mine), near(other))
-    return jnp.transpose(out, (0, 1, 2, 4, 3))
+    return jnp.transpose(jnp.reshape(out, (slices_all, entries, 4, 2, 4)), (0, 1, 2, 4, 3))
 
 
 def solution(mesh):

time: 16.6 us -> 16.5 us (level)
  no operation moved by 1% of the time
where the time goes in v6:
time: 16.5 us; the launch traced here: 16.3 us
  blocking collectives  9.45 us (57%)
  Pallas kernels  2.81 us (17%)
  starting transfers between devices  2.7 us (16%)
  waiting for transfers between devices  1.37 us (8%)
    all_to_all x1, blocking collectives, body(): parts = lax.all_to_all(copies, axes, 0, 0, axis_index_groups=groups)  9.45 us
    ppermute x1, starting transfers between devices, from_behind(): lax.ppermute(array, axis, [(i, (i + by) % peers) for i in range(peers)])  2.43 us
    pallas_call x1, Pallas kernels, body(): pl.pallas_call(lambda *refs: first_kernel(slices, (slices_all, depth_coun...  1.84 us
    ppermute x1, waiting for transfers between devices, body(): other = lax.ppermute(mine, 'gz', [(i, i ^ 1) for i in range(sizes[1])])  0.91 us
    pallas_call x1, Pallas kernels, body(): pl.pallas_call(lambda *refs: final_kernel(slices, results, [chip[0] for c...  0.69 us
    ppermute x1, waiting for transfers between devices, from_behind(): lax.ppermute(array, axis, [(i, (i + by) % peers) for i in range(peers)])  0.46 us
  transfers between devices with their start and end apart: 2, of which 2 were waited for; matrix products, arithmetic and copies ran while one was open for 0% of the time, Pallas kernels for 11%

profile of v6, /device:TPU:0, one launch (start us, length us, event | category | flops | bytes accessed | tf_op | source)
XLA Modules:
  0.0 16.3 jit_solution(8393681604399713765)
XLA Ops:
  0.0 2.4 %collective-permute-start = (bf16[288,128]{1,0:T(8,128)(2,1)}, bf16[288,128]{1,0:T(8,128)(2,1)S(1)}, u32[]{:S(2)}, u32[]{:S(2)}) collective-permute-start(bf16[288,128]{1,0:T(8,128)(2,1)} %bitcast.16), channel_id=1, source_target_pairs={{0,12},{4,0},{8,4},{12,8},{1,13},{5,1},{9,5},{13,9},{2,14},{6,2},{... | collective-permute-start | bytes 221192 | tf_op jit(solution)/shard_map/ppermute | solution.py:281
  2.4 1.8 %local.1 = (f32[2560,128]{1,0:T(8,128)S(1)}, f32[8,128]{1,0:T(8,128)S(1)}, f32[24,128]{1,0:T(8,128)S(1)}, f32[18,128]{1,0:T(8,128)}) custom-call(s32[2,4]{1,0:T(2,128)} %refs_0_.1, s32[3]{0:T(128)} %refs_1_.1, s32[4]{0:T(128)} %refs_2_.1, s32[4,4]{1,0:T(4,128)} %refs_3_.1, s32[4,4]{1,0:T(4,128)} %refs_4_.1, bf16[288,128]{1,0:T(8,128)(2,1)} %bitcast.17, ...), custom_call_target="tpu_custom_call" | custom-call | tf_op jit(solution)/shard_map/local/pallas_call | solution.py:305
  4.3 0.5 %collective-permute-done.refs_1_ = bf16[288,128]{1,0:T(8,128)(2,1)S(1)} collective-permute-done((bf16[288,128]{1,0:T(8,128)(2,1)}, bf16[288,128]{1,0:T(8,128)(2,1)S(1)}, u32[]{:S(2)}, u32[]{:S(2)}) %collective-permute-start) | collective-permute-done | bytes 73760 | tf_op jit(solution)/shard_map/ppermute | solution.py:281
  4.7 0.3 %last.1 = f32[1,128]{1,0:T(1,128)S(1)} custom-call(f32[2560,128]{1,0:T(8,128)S(1)} %get-tuple-element.8.refs_0_, bf16[288,128]{1,0:T(8,128)(2,1)S(1)} %collective-permute-done.refs_1_, f32[24,128]{1,0:T(8,128)S(1)} %get-tuple-element.9.refs_2_, f32[8,128]{1,0:T(8,128)S(1)} %get-tuple-element.10.refs_3_), custom_call_target="tpu_custom_call" | custom-call | tf_op jit(solution)/shard_map/last/pallas_call | solution.py:335
  5.0 9.5 %all_to_all.5 = f32[16,1,128]{2,1,0:T(1,128)S(1)} all-to-all(f32[16,1,128]{2,1,0:T(1,128)S(1)} %broadcast_in_dim.9), channel_id=1, replica_groups={{27,19,26,18,25,17,24,16,11,3,10,2,9,1,8,0},{31,23,30,22,29,21,28,20,15..., dimensions={0} | all-to-all | bytes 16384 | tf_op jit(solution)/shard_map/all_to_all | solution.py:346
  14.5 0.3 %collective-permute-start.1 = (f32[16,128]{1,0:T(8,128)S(1)}, f32[16,128]{1,0:T(8,128)S(1)}, u32[]{:S(2)}, u32[]{:S(2)}) collective-permute-start(f32[16,128]{1,0:T(8,128)S(1)} %bitcast.13), channel_id=1, source_target_pairs={{0,4},{4,0},{8,12},{12,8},{1,5},{5,1},{9,13},{13,9},{2,6},{6,2},{1... | collective-permute-start | bytes 24584 | tf_op jit(solution)/shard_map/ppermute | solution.py:348
  14.7 0.9 %collective-permute-done.1.refs_1_ = f32[16,128]{1,0:T(8,128)S(1)} collective-permute-done((f32[16,128]{1,0:T(8,128)S(1)}, f32[16,128]{1,0:T(8,128)S(1)}, u32[]{:S(2)}, u32[]{:S(2)}) %collective-permute-start.1) | collective-permute-done | bytes 8224 | tf_op jit(solution)/shard_map/ppermute | solution.py:348
  15.6 0.7 %final.1 = f32[48,4]{1,0:T(8,128)} custom-call(f32[16,128]{1,0:T(8,128)S(1)} %bitcast.14, f32[16,128]{1,0:T(8,128)S(1)} %collective-permute-done.1.refs_1_), custom_call_target="tpu_custom_call" | custom-call | tf_op jit(solution)/shard_map/final/pallas_call | solution.py:350
  (1 shorter events, 0.0 us)
Async XLA Ops:
  0.0 4.7 %collective-permute-start = (bf16[288,128]{1,0:T(8,128)(2,1)}, bf16[288,128]{1,0:T(8,128)(2,1)S(1)}, u32[]{:S(2)}, u32[]{:S(2)}) collective-permute-start(bf16[288,128]{1,0:T(8,128)(2,1)} %bitcast.16), channel_id=1, source_target_pairs={{0,12},{4,0},{8,4},{12,8},{1,13},{5,1},{9,5},{13,9},{2,14},{6,2},{... | collective-permute-start | bytes 221192 | tf_op jit(solution)/shard_map/ppermute | solution.py:281
  14.5 1.2 %collective-permute-start.1 = (f32[16,128]{1,0:T(8,128)S(1)}, f32[16,128]{1,0:T(8,128)S(1)}, u32[]{:S(2)}, u32[]{:S(2)}) collective-permute-start(f32[16,128]{1,0:T(8,128)S(1)} %bitcast.13), channel_id=1, source_target_pairs={{0,4},{4,0},{8,12},{12,8},{1,5},{5,1},{9,13},{13,9},{2,6},{6,2},{1... | collective-permute-start | bytes 24584 | tf_op jit(solution)/shard_map/ppermute | solution.py:348

commit v7 on v6

v7 whole, which is shorter than its diff:
```python
import math

import jax
import jax.numpy as jnp
from jax import lax
from jax.experimental import pallas as pl
from jax.experimental.pallas import tpu as pltpu
from jax.sharding import PartitionSpec as P

f32 = jnp.float32
LANES = 128
PAD = 40


def vmem(count):
    return [pl.BlockSpec(memory_space=pltpu.VMEM) for _ in range(count)]


def near(array):
    return pltpu.with_memory_space_constraint(array, pltpu.VMEM)


def kept(shape):
    return pltpu.VMEM(shape, f32)


def smem(count):
    return [pl.BlockSpec(memory_space=pltpu.SMEM) for _ in range(count)]


def widen(packed_ref, wide_ref):
    rows = packed_ref.shape[0]
    wide_ref[0:rows, :] = packed_ref[...].astype(f32)
    wide_ref[rows:, :] = jnp.zeros((wide_ref.shape[0] - rows, wide_ref.shape[1]), f32)


def strided(wide_ref, part, spin, first, count, slices, now):
    start = ((part * 36 + first) * slices + now) * 4 + spin
    return wide_ref[pl.ds(start, count, stride=4 * slices), :]


def pair_rows(left_ref, wide_ref, slices, now):
    tiles = []
    for u in range(4):
        sums = [None] * 8
        for j in range(PAD // 8):
            rr = strided(wide_ref, 0, u, 8 * j, 8, slices, now)
            ri = strided(wide_ref, 1, u, 8 * j, 8, slices, now)
            for s in range(4):
                lr = left_ref[pl.ds((now * 8 + s) * PAD + 8 * j, 8), :]
                li = left_ref[pl.ds((now * 8 + 4 + s) * PAD + 8 * j, 8), :]
                re = lr * rr - li * ri
                im = lr * ri + li * rr
                sums[s] = re if j == 0 else sums[s] + re
                sums[s + 4] = im if j == 0 else sums[s + 4] + im
        tiles.append(fold(sums))
    return tiles


def weighed(tiles, table):
    total = None
    for u, tile in enumerate(tiles):
        part = jnp.sum(tile, axis=1, keepdims=True) * table[u]
        total = part if total is None else total + part
    return jnp.sum(total, axis=0, keepdims=True)


def left_rows(left_ref, now, part, s, first, value):
    left_ref[pl.ds((now * 8 + part * 4 + s) * PAD + first, value.shape[0]), :] = value


def dressed(left_ref, wide_ref, wilson, slices, now):
    zeros = jnp.zeros((PAD - 36, left_ref.shape[1]), f32)
    for s in range(4):
        for b in range(3):
            real = imag = None
            for a in range(3):
                sr = strided(wide_ref, 0, s, a * 12, 12, slices, now)
                si = strided(wide_ref, 1, s, a * 12, 12, slices, now)
                wr, wi = wilson(0, a, b), wilson(1, a, b)
                re = sr * wr + si * wi
                im = sr * wi - si * wr
                real = re if real is None else real + re
                imag = im if imag is None else imag + im
            left_rows(left_ref, now, 0, s, b * 12, real)
            left_rows(left_ref, now, 1, s, b * 12, imag)
        left_rows(left_ref, now, 0, s, 36, zeros)
        left_rows(left_ref, now, 1, s, 36, zeros)


def fold(tiles):
    row = lax.broadcasted_iota(jnp.int32, tiles[0].shape, 0)
    for bit in (4, 2, 1):
        half = len(tiles) // 2
        low = row & bit == 0
        tiles = [
            jnp.where(low, a + pltpu.roll(a, 8 - bit, 0), b + pltpu.roll(b, bit, 0)) for a, b in zip(tiles[:half], tiles[half:])
        ]
    return tiles[0]


def fill_tables(sizes, scaling, slices, entries, now, source_ref, entry_ref, momenta_ref, perm_ref, turn_ref):
    depth_count = sizes[1]
    nsteps = (entries - 1) // 2
    depth, first_slice = lax.axis_index("gz"), lax.axis_index("ta") * slices
    tables = [[[] for _ in range(4)] for _ in range(nsteps + 1)]
    for row in range(-(-entries * 32 // LANES)):
        lane = lax.broadcasted_iota(jnp.int32, (8, LANES), 1)
        sub = lax.broadcasted_iota(jnp.int32, (8, LANES), 0)
        turned = 31 - lane // 4
        slot, to_imag, lane_p = row * 16 + turned // 2, turned % 2 == 1, lane % 4
        insertion, from_imag, spin = slot % 4, sub >= 4, sub % 4
        offset = jnp.full((8, LANES), -1, jnp.int32)
        for j in range(entries):
            offset = jnp.where(slot // 4 == j, entry_ref[j], offset)
        momentum = origin = jnp.zeros((8, LANES), jnp.int32)
        for p in range(4):
            momentum = jnp.where(lane_p == p, momenta_ref[p], momentum)
            origin = jnp.where(lane_p == p, source_ref[first_slice + now, p], origin)
        ahead = jnp.maximum(nsteps - offset, 0)
        angle = lax.rem(momentum * (depth + ahead + depth_count - origin), depth_count).astype(f32) * (2.0 * math.pi / depth_count)
        cosine, sine = jnp.cos(angle) * scaling, jnp.sin(angle) * scaling

        def turned_phase(turn):
            real = jnp.where(turn == 0, cosine, jnp.where(turn == 1, sine, jnp.where(turn == 2, -cosine, -sine)))
            imag = jnp.where(turn == 0, -sine, jnp.where(turn == 1, cosine, jnp.where(turn == 2, sine, -cosine)))
            return real, imag

        def by_insertion(ref, s):
            value = jnp.zeros((8, LANES), jnp.int32)
            for g in range(4):
                value = jnp.where(insertion == g, ref[g, s], value)
            return value

        columns, turns = [by_insertion(perm_ref, s) for s in range(4)], [by_insertion(turn_ref, s) for s in range(4)]
        own_column = own_turn = jnp.zeros((8, LANES), jnp.int32)
        for s in range(4):
            own_column = jnp.where(spin == s, columns[s], own_column)
            own_turn = jnp.where(spin == s, turns[s], own_turn)
        real, imag = turned_phase(own_turn)
        plain = jnp.where(to_imag, jnp.where(from_imag, real, imag), jnp.where(from_imag, -imag, real))
        for u in range(4):
            real, imag = turned_phase(turns[u])
            mirrored = jnp.where(to_imag, jnp.where(from_imag, -real, imag), jnp.where(from_imag, imag, real))
            for reach in range(nsteps + 1):
                weight = jnp.where((offset == nsteps + reach) & (own_column == u), plain, 0.0)
                if reach:
                    weight = jnp.where((offset == nsteps - reach) & (columns[u] == spin), mirrored, weight)
                tables[reach][u].append(weight)
    return tables


def first_kernel(slices, sizes, scaling, entries, source_z_ref, entry_ref, momenta_ref, perm_ref, turn_ref, source_ref, links_ref,
                 left_ref, begun_ref, tables_ref, wilson_ref, wide_ref, plain_ref):
    widen(source_ref, wide_ref)
    zeros = jnp.zeros((PAD - 36, LANES), f32)
    nsteps = (entries - 1) // 2
    width = begun_ref.shape[1] // slices
    for now in range(slices):
        tables = fill_tables(sizes, scaling, slices, entries, now, source_z_ref, entry_ref, momenta_ref, perm_ref, turn_ref)
        for reach in range(1, nsteps + 1):
            for u in range(4):
                for row, weight in enumerate(tables[reach][u]):
                    at = ((now * nsteps + reach - 1) * 4 + u) * 8
                    tables_ref[at : at + 8, row * LANES : (row + 1) * LANES] = weight
        for s in range(4):
            left_rows(plain_ref, now, 0, s, 0, strided(wide_ref, 0, s, 0, 36, slices, now))
            left_rows(plain_ref, now, 1, s, 0, -strided(wide_ref, 1, s, 0, 36, slices, now))
            left_rows(plain_ref, now, 0, s, 36, zeros)
            left_rows(plain_ref, now, 1, s, 36, zeros)
        tiles = pair_rows(plain_ref, wide_ref, slices, now)
        for row in range(width // LANES):
            at = now * width + row * LANES
            begun_ref[:, at : at + LANES] = weighed(tiles, [tables[0][u][row] for u in range(4)])
        for part in range(2):
            for a in range(3):
                for b in range(3):
                    wilson_ref[pl.ds((now * 2 + part) * 9 + a * 3 + b, 1), :] = links_ref[a, b, now, part : part + 1, :].astype(f32)
        dressed(left_ref, wide_ref, lambda part, a, b: wilson_ref[pl.ds((now * 2 + part) * 9 + a * 3 + b, 1), :], slices, now)


def further_kernel(slices, source_ref, moved_ref, before_ref, left_ref, wilson_ref, wide_ref):
    widen(source_ref, wide_ref)
    for now in range(slices):
        def link(part, a, b):
            return moved_ref[a, b, now, part : part + 1, :].astype(f32)

        def old(part, a, b):
            return before_ref[pl.ds((now * 2 + part) * 9 + a * 3 + b, 1), :]

        for a in range(3):
            for b in range(3):
                real = sum(old(0, a, m) * link(0, m, b) - old(1, a, m) * link(1, m, b) for m in range(3))
                imag = sum(old(0, a, m) * link(1, m, b) + old(1, a, m) * link(0, m, b) for m in range(3))
                wilson_ref[pl.ds(now * 18 + a * 3 + b, 1), :] = real
                wilson_ref[pl.ds(now * 18 + 9 + a * 3 + b, 1), :] = imag
        dressed(left_ref, wide_ref, lambda part, a, b: wilson_ref[pl.ds((now * 2 + part) * 9 + a * 3 + b, 1), :], slices, now)


def pairs_kernel(slices, nsteps, reach, left_ref, moved_ref, tables_ref, begun_ref, out_ref, wide_ref):
    widen(moved_ref, wide_ref)
    width = tables_ref.shape[1]
    for now in range(slices):
        tiles = pair_rows(left_ref, wide_ref, slices, now)
        first = (now * nsteps + reach - 1) * 32
        table = [tables_ref[first + 8 * u : first + 8 * u + 8, :] for u in range(4)]
        row = begun_ref[:, now * width : (now + 1) * width] + weighed(tiles, table)
        out_ref[:, now * width : (now + 1) * width] = jnp.broadcast_to(row, (out_ref.shape[0], width))


def final_kernel(slices, rows, owners, mine_ref, other_ref, out_ref):
    sections = out_ref.shape[0] // (slices * rows)
    each = len(owners) // sections
    width = mine_ref.shape[1] // slices
    for place in range(sections):
        picked = slice(place * each, (place + 1) * each)
        total = jnp.sum(mine_ref[picked, :] + other_ref[picked, :], axis=0, keepdims=True)
        for now in range(slices):
            for block in range(rows // 8):
                at = now * width + block // 4 * LANES
                tile = jnp.broadcast_to(total[:, at : at + LANES], (8, LANES))
                tile = pltpu.roll(tile, 4 + 32 * (block % 4), 1, stride=4, stride_axis=0)
                first = (owners[place * each] * slices + now) * rows + block * 8
                out_ref[first : first + 8, :] = tile[:, 0:4]


def chips_and_groups(sizes):
    nt, nz, ny = sizes
    chips = [(t, b, y) for t in range(nt) for b in range(nz // 2) for y in range(ny)]
    corner = chips[-1]
    chips.sort(key=lambda chip: (-chip[0], sum(abs(i - j) for i, j in zip(chip, corner)), chip))
    groups = [[(t * nz + 2 * b + half) * ny + y for t, b, y in chips] for half in range(2)]
    return chips, groups


def from_behind(array, axis, by):
    peers = lax.axis_size(axis)
    return lax.ppermute(array, axis, [(i, (i + by) % peers) for i in range(peers)])


def body(propagator, links, source_z, displacements, momenta, gamma_perm, gamma_phase):
    axes = ("ta", "gz", "gy")
    sizes = tuple(lax.axis_size(a) for a in axes)
    depth_count = sizes[1]
    entries = displacements.shape[0]
    nsteps = (entries - 1) // 2
    slices = propagator.shape[4]
    sites = propagator.shape[6]
    slices_all = slices * sizes[0]
    scaling = 1.0 / (24.0 * math.sqrt(sites * sizes[2] * depth_count))
    source = jnp.reshape(jnp.transpose(propagator, (0, 2, 3, 4, 5, 1, 6)), (288 * slices, sites))
    linked = jnp.reshape(jnp.transpose(links, (1, 2, 3, 4, 0, 5)), (3, 3, slices, 2, sites))
    moved, moved_links = source, linked
    wide = pltpu.VMEM((288 * slices + 16 * slices, sites), f32)
    plain = pltpu.VMEM((slices * 8 * PAD, sites), f32)
    rows = -(-entries * 32 // LANES)
    width = rows * LANES

    moved = from_behind(moved, "gz", -1)
    chips, groups = chips_and_groups(sizes)
    shape_left = kept((slices * 8 * PAD, sites))
    shape_wilson = kept((slices * 18, sites))
    left, total, tables, wilson = pl.pallas_call(
        lambda *refs: first_kernel(slices, (slices_all, depth_count), scaling, entries, *refs),
        out_shape=(shape_left, kept((1, slices * width)), kept((slices * nsteps * 32, width)), shape_wilson),
        in_specs=smem(5) + vmem(2),
        out_specs=tuple(vmem(4)),
        scratch_shapes=[wide, plain],
        name="local",
    )(source_z, displacements, momenta, gamma_perm, gamma_phase, source, linked)
    for reach in range(1, nsteps + 1):
        total = pl.pallas_call(
            lambda *refs, reach=reach: pairs_kernel(slices, nsteps, reach, *refs),
            out_shape=kept((len(chips) if reach == nsteps else 1, slices * width)),
            in_specs=vmem(4),
            out_specs=vmem(1)[0],
            scratch_shapes=[wide],
            name="pairs",
        )(near(left), near(moved), near(tables), near(total))
        if reach < nsteps:
            moved_links = from_behind(moved_links, "gz", -1)
            moved = from_behind(moved, "gz", -1)
            left, wilson = pl.pallas_call(
                lambda *refs: further_kernel(slices, *refs),
                out_shape=(shape_left, shape_wilson),
                in_specs=vmem(3),
                out_specs=tuple(vmem(2)),
                scratch_shapes=[wide],
                name="further",
            )(source, moved_links, near(wilson))
    parts = lax.all_to_all(jnp.reshape(total, (len(chips), 1, slices * width)), axes, 0, 0, axis_index_groups=groups)
    mine = jnp.reshape(parts, (len(chips), slices * width))
    other = lax.ppermute(mine, "gz", [(i, i ^ 1) for i in range(sizes[1])])
    results = entries * 8
    out = pl.pallas_call(
        lambda *refs: final_kernel(slices, results, [chip[0] for chip in chips], *refs),
        out_shape=jax.ShapeDtypeStruct((slices_all * results, 4), f32),
        in_specs=vmem(2),
        name="final",
    )(near(mine), near(other))
    return jnp.transpose(jnp.reshape(out, (slices_all, entries, 4, 2, 4)), (0, 1, 2, 4, 3))


def solution(mesh):
    placed = (
        P(None, None, None, None, "ta", "gz", "gy"),
        P(None, None, None, "ta", "gz", "gy"),
        P(),
        P(),
        P(),
        P(),
        P(),
    )
    return jax.shard_map(body, mesh=mesh, in_specs=placed, out_specs=P(), check_vma=False)
```

time: 16.5 us -> 16.4 us (level)
  Pallas kernels: 2.81 us -> 2.58 us
  transfers between devices with their start and end apart: 2 -> 2, of which waited for: 2 -> 2; matrix products, arithmetic and copies ran while one was open for 0% -> 0% of each run, Pallas kernels for 11% -> 10%
where the time goes in v7:
time: 16.4 us; the launch traced here: 16.2 us
  blocking collectives  9.44 us (58%)
  starting transfers between devices  2.7 us (16%)
  Pallas kernels  2.58 us (16%)
  waiting for transfers between devices  1.52 us (9%)
    all_to_all x1, blocking collectives, body(): lax.all_to_all(jnp.reshape(total, (len(chips), 1, slices * width)), axes,...  9.44 us
    ppermute x1, starting transfers between devices, from_behind(): lax.ppermute(array, axis, [(i, (i + by) % peers) for i in range(peers)])  2.43 us
    pallas_call x1, Pallas kernels, body(): pl.pallas_call(lambda *refs: first_kernel(slices, (slices_all, depth_coun...  1.69 us
    ppermute x1, waiting for transfers between devices, body(): other = lax.ppermute(mine, 'gz', [(i, i ^ 1) for i in range(sizes[1])])  0.91 us
    pallas_call x1, Pallas kernels, body(): pl.pallas_call(lambda *refs: final_kernel(slices, results, [chip[0] for c...  0.69 us
    ppermute x1, waiting for transfers between devices, from_behind(): lax.ppermute(array, axis, [(i, (i + by) % peers) for i in range(peers)])  0.61 us
  transfers between devices with their start and end apart: 2, of which 2 were waited for; matrix products, arithmetic and copies ran while one was open for 0% of the time, Pallas kernels for 10%

profile of v7, /device:TPU:0, one launch (start us, length us, event | category | flops | bytes accessed | tf_op | source)
XLA Modules:
  0.0 16.2 jit_solution(3192323904970666894)
XLA Ops:
  0.0 2.4 %collective-permute-start = (bf16[288,128]{1,0:T(8,128)(2,1)}, bf16[288,128]{1,0:T(8,128)(2,1)S(1)}, u32[]{:S(2)}, u32[]{:S(2)}) collective-permute-start(bf16[288,128]{1,0:T(8,128)(2,1)} %bitcast.18), channel_id=1, source_target_pairs={{0,12},{4,0},{8,4},{12,8},{1,13},{5,1},{9,5},{13,9},{2,14},{6,2},{... | collective-permute-start | bytes 221192 | tf_op jit(solution)/shard_map/ppermute | solution.py:238
  2.4 1.7 %local.1 = (f32[320,128]{1,0:T(8,128)S(1)}, f32[1,128]{1,0:T(1,128)S(1)}, f32[32,128]{1,0:T(8,128)S(1)}, f32[18,128]{1,0:T(8,128)}) custom-call(s32[2,4]{1,0:T(2,128)} %refs_0_.1, s32[3]{0:T(128)} %refs_1_.1, s32[4]{0:T(128)} %refs_2_.1, s32[4,4]{1,0:T(4,128)} %refs_3_.1, s32[4,4]{1,0:T(4,128)} %refs_4_.1, bf16[288,128]{1,0:T(8,128)(2,1)} %bitcast.19, ...), custom_call_target="tpu_custom_call" | custom-call | tf_op jit(solution)/shard_map/local/pallas_call | solution.py:263
  4.1 0.6 %collective-permute-done.refs_1_ = bf16[288,128]{1,0:T(8,128)(2,1)S(1)} collective-permute-done((bf16[288,128]{1,0:T(8,128)(2,1)}, bf16[288,128]{1,0:T(8,128)(2,1)S(1)}, u32[]{:S(2)}, u32[]{:S(2)}) %collective-permute-start) | collective-permute-done | bytes 73760 | tf_op jit(solution)/shard_map/ppermute | solution.py:238
  4.7 0.2 %pairs.1 = f32[16,128]{1,0:T(8,128)S(1)} custom-call(f32[320,128]{1,0:T(8,128)S(1)} %get-tuple-element.8.refs_0_, bf16[288,128]{1,0:T(8,128)(2,1)S(1)} %collective-permute-done.refs_1_, f32[32,128]{1,0:T(8,128)S(1)} %get-tuple-element.9.refs_2_, f32[1,128]{1,0:T(1,128)S(1)} %get-tuple-element.10.refs_3_), custom_call_target="tpu_custom_call" | custom-call | tf_op jit(solution)/shard_map/pairs/pallas_call | solution.py:272
  4.9 9.4 %all_to_all.5 = f32[16,1,128]{2,1,0:T(1,128)S(1)} all-to-all(f32[16,1,128]{2,1,0:T(1,128)S(1)} %bitcast.17), channel_id=1, replica_groups={{27,19,26,18,25,17,24,16,11,3,10,2,9,1,8,0},{31,23,30,22,29,21,28,20,15..., dimensions={0} | all-to-all | bytes 16384 | tf_op jit(solution)/shard_map/all_to_all | solution.py:291
  14.4 0.3 %collective-permute-start.1 = (f32[16,128]{1,0:T(8,128)S(1)}, f32[16,128]{1,0:T(8,128)S(1)}, u32[]{:S(2)}, u32[]{:S(2)}) collective-permute-start(f32[16,128]{1,0:T(8,128)S(1)} %bitcast.15), channel_id=1, source_target_pairs={{0,4},{4,0},{8,12},{12,8},{1,5},{5,1},{9,13},{13,9},{2,6},{6,2},{1... | collective-permute-start | bytes 24584 | tf_op jit(solution)/shard_map/ppermute | solution.py:293
  14.6 0.9 %collective-permute-done.1.refs_1_ = f32[16,128]{1,0:T(8,128)S(1)} collective-permute-done((f32[16,128]{1,0:T(8,128)S(1)}, f32[16,128]{1,0:T(8,128)S(1)}, u32[]{:S(2)}, u32[]{:S(2)}) %collective-permute-start.1) | collective-permute-done | bytes 8224 | tf_op jit(solution)/shard_map/ppermute | solution.py:293
  15.6 0.7 %final.1 = f32[48,4]{1,0:T(8,128)} custom-call(f32[16,128]{1,0:T(8,128)S(1)} %bitcast.16, f32[16,128]{1,0:T(8,128)S(1)} %collective-permute-done.1.refs_1_), custom_call_target="tpu_custom_call" | custom-call | tf_op jit(solution)/shard_map/final/pallas_call | solution.py:295
Async XLA Ops:
  0.0 4.7 %collective-permute-start = (bf16[288,128]{1,0:T(8,128)(2,1)}, bf16[288,128]{1,0:T(8,128)(2,1)S(1)}, u32[]{:S(2)}, u32[]{:S(2)}) collective-permute-start(bf16[288,128]{1,0:T(8,128)(2,1)} %bitcast.18), channel_id=1, source_target_pairs={{0,12},{4,0},{8,4},{12,8},{1,13},{5,1},{9,5},{13,9},{2,14},{6,2},{... | collective-permute-start | bytes 221192 | tf_op jit(solution)/shard_map/ppermute | solution.py:238
  14.4 1.2 %collective-permute-start.1 = (f32[16,128]{1,0:T(8,128)S(1)}, f32[16,128]{1,0:T(8,128)S(1)}, u32[]{:S(2)}, u32[]{:S(2)}) collective-permute-start(f32[16,128]{1,0:T(8,128)S(1)} %bitcast.15), channel_id=1, source_target_pairs={{0,4},{4,0},{8,12},{12,8},{1,5},{5,1},{9,13},{13,9},{2,6},{6,2},{1... | collective-permute-start | bytes 24584 | tf_op jit(solution)/shard_map/ppermute | solution.py:293

commit v8 on v7

--- a/solution.py
+++ b/solution.py
@@ -227,9 +227,12 @@
 def chips_and_groups(sizes):
     nt, nz, ny = sizes
     chips = [(t, b, y) for t in range(nt) for b in range(nz // 2) for y in range(ny)]
-    corner = chips[-1]
-    chips.sort(key=lambda chip: (-chip[0], sum(abs(i - j) for i, j in zip(chip, corner)), chip))
-    groups = [[(t * nz + 2 * b + half) * ny + y for t, b, y in chips] for half in range(2)]
+    groups = []
+    for half in range(2):
+        t, b, y = max(chips)
+        leader = (t, b, max(y - half, 0))
+        chips.sort(key=lambda chip: (-chip[0], sum(abs(i - j) for i, j in zip(chip, leader)), chip))
+        groups.append([(t * nz + 2 * b + half) * ny + y for t, b, y in chips])
     return chips, groups
 
 

time: 16.4 us -> 16.4 us (level)
  no operation moved by 1% of the time
where the time goes in v8:
time: 16.4 us; the launch traced here: 16.2 us
  blocking collectives  9.44 us (58%)
  starting transfers between devices  2.61 us (16%)
  Pallas kernels  2.58 us (16%)
  waiting for transfers between devices  1.61 us (10%)
    all_to_all x1, blocking collectives, body(): lax.all_to_all(jnp.reshape(total, (len(chips), 1, slices * width)), axes,...  9.44 us
    ppermute x1, starting transfers between devices, from_behind(): lax.ppermute(array, axis, [(i, (i + by) % peers) for i in range(peers)])  2.43 us
    pallas_call x1, Pallas kernels, body(): pl.pallas_call(lambda *refs: first_kernel(slices, (slices_all, depth_coun...  1.69 us
    ppermute x1, waiting for transfers between devices, body(): other = lax.ppermute(mine, 'gz', [(i, i ^ 1) for i in range(sizes[1])])  1 us
    pallas_call x1, Pallas kernels, body(): pl.pallas_call(lambda *refs: final_kernel(slices, results, [chip[0] for c...  0.69 us
    ppermute x1, waiting for transfers between devices, from_behind(): lax.ppermute(array, axis, [(i, (i + by) % peers) for i in range(peers)])  0.61 us
  transfers between devices with their start and end apart: 2, of which 2 were waited for; matrix products, arithmetic and copies ran while one was open for 0% of the time, Pallas kernels for 10%

profile of v8, /device:TPU:0, one launch (start us, length us, event | category | flops | bytes accessed | tf_op | source)
XLA Modules:
  0.0 16.2 jit_solution(311196389609903244)
XLA Ops:
  0.0 2.4 %collective-permute-start = (bf16[288,128]{1,0:T(8,128)(2,1)}, bf16[288,128]{1,0:T(8,128)(2,1)S(1)}, u32[]{:S(2)}, u32[]{:S(2)}) collective-permute-start(bf16[288,128]{1,0:T(8,128)(2,1)} %bitcast.18), channel_id=1, source_target_pairs={{0,12},{4,0},{8,4},{12,8},{1,13},{5,1},{9,5},{13,9},{2,14},{6,2},{... | collective-permute-start | bytes 221192 | tf_op jit(solution)/shard_map/ppermute | solution.py:241
  2.4 1.7 %local.1 = (f32[320,128]{1,0:T(8,128)S(1)}, f32[1,128]{1,0:T(1,128)S(1)}, f32[32,128]{1,0:T(8,128)S(1)}, f32[18,128]{1,0:T(8,128)}) custom-call(s32[2,4]{1,0:T(2,128)} %refs_0_.1, s32[3]{0:T(128)} %refs_1_.1, s32[4]{0:T(128)} %refs_2_.1, s32[4,4]{1,0:T(4,128)} %refs_3_.1, s32[4,4]{1,0:T(4,128)} %refs_4_.1, bf16[288,128]{1,0:T(8,128)(2,1)} %bitcast.19, ...), custom_call_target="tpu_custom_call" | custom-call | tf_op jit(solution)/shard_map/local/pallas_call | solution.py:266
  4.1 0.6 %collective-permute-done.refs_1_ = bf16[288,128]{1,0:T(8,128)(2,1)S(1)} collective-permute-done((bf16[288,128]{1,0:T(8,128)(2,1)}, bf16[288,128]{1,0:T(8,128)(2,1)S(1)}, u32[]{:S(2)}, u32[]{:S(2)}) %collective-permute-start) | collective-permute-done | bytes 73760 | tf_op jit(solution)/shard_map/ppermute | solution.py:241
  4.7 0.2 %pairs.1 = f32[16,128]{1,0:T(8,128)S(1)} custom-call(f32[320,128]{1,0:T(8,128)S(1)} %get-tuple-element.8.refs_0_, bf16[288,128]{1,0:T(8,128)(2,1)S(1)} %collective-permute-done.refs_1_, f32[32,128]{1,0:T(8,128)S(1)} %get-tuple-element.9.refs_2_, f32[1,128]{1,0:T(1,128)S(1)} %get-tuple-element.10.refs_3_), custom_call_target="tpu_custom_call" | custom-call | tf_op jit(solution)/shard_map/pairs/pallas_call | solution.py:275
  4.9 9.4 %all_to_all.5 = f32[16,1,128]{2,1,0:T(1,128)S(1)} all-to-all(f32[16,1,128]{2,1,0:T(1,128)S(1)} %bitcast.17), channel_id=1, replica_groups={{27,19,26,18,25,17,24,16,11,3,10,2,9,1,8,0},{30,22,29,31,21,23,28,20,14..., dimensions={0} | all-to-all | bytes 16384 | tf_op jit(solution)/shard_map/all_to_all | solution.py:294
  14.4 0.2 %collective-permute-start.1 = (f32[16,128]{1,0:T(8,128)S(1)}, f32[16,128]{1,0:T(8,128)S(1)}, u32[]{:S(2)}, u32[]{:S(2)}) collective-permute-start(f32[16,128]{1,0:T(8,128)S(1)} %bitcast.15), channel_id=1, source_target_pairs={{0,4},{4,0},{8,12},{12,8},{1,5},{5,1},{9,13},{13,9},{2,6},{6,2},{1... | collective-permute-start | bytes 24584 | tf_op jit(solution)/shard_map/ppermute | solution.py:296
  14.6 1.0 %collective-permute-done.1.refs_1_ = f32[16,128]{1,0:T(8,128)S(1)} collective-permute-done((f32[16,128]{1,0:T(8,128)S(1)}, f32[16,128]{1,0:T(8,128)S(1)}, u32[]{:S(2)}, u32[]{:S(2)}) %collective-permute-start.1) | collective-permute-done | bytes 8224 | tf_op jit(solution)/shard_map/ppermute | solution.py:296
  15.6 0.7 %final.1 = f32[48,4]{1,0:T(8,128)} custom-call(f32[16,128]{1,0:T(8,128)S(1)} %bitcast.16, f32[16,128]{1,0:T(8,128)S(1)} %collective-permute-done.1.refs_1_), custom_call_target="tpu_custom_call" | custom-call | tf_op jit(solution)/shard_map/final/pallas_call | solution.py:298
Async XLA Ops:
  0.0 4.7 %collective-permute-start = (bf16[288,128]{1,0:T(8,128)(2,1)}, bf16[288,128]{1,0:T(8,128)(2,1)S(1)}, u32[]{:S(2)}, u32[]{:S(2)}) collective-permute-start(bf16[288,128]{1,0:T(8,128)(2,1)} %bitcast.18), channel_id=1, source_target_pairs={{0,12},{4,0},{8,4},{12,8},{1,13},{5,1},{9,5},{13,9},{2,14},{6,2},{... | collective-permute-start | bytes 221192 | tf_op jit(solution)/shard_map/ppermute | solution.py:241
  14.4 1.2 %collective-permute-start.1 = (f32[16,128]{1,0:T(8,128)S(1)}, f32[16,128]{1,0:T(8,128)S(1)}, u32[]{:S(2)}, u32[]{:S(2)}) collective-permute-start(f32[16,128]{1,0:T(8,128)S(1)} %bitcast.15), channel_id=1, source_target_pairs={{0,4},{4,0},{8,12},{12,8},{1,5},{5,1},{9,13},{13,9},{2,6},{6,2},{1... | collective-permute-start | bytes 24584 | tf_op jit(solution)/shard_map/ppermute | solution.py:296

commit v9 on v7

--- a/solution.py
+++ b/solution.py
@@ -42,17 +42,17 @@
 def pair_rows(left_ref, wide_ref, slices, now):
     tiles = []
     for u in range(4):
-        sums = [None] * 8
+        sums = [None] * 12
         for j in range(PAD // 8):
             rr = strided(wide_ref, 0, u, 8 * j, 8, slices, now)
             ri = strided(wide_ref, 1, u, 8 * j, 8, slices, now)
+            factors = (ri - rr, rr + ri, rr)
             for s in range(4):
-                lr = left_ref[pl.ds((now * 8 + s) * PAD + 8 * j, 8), :]
-                li = left_ref[pl.ds((now * 8 + 4 + s) * PAD + 8 * j, 8), :]
-                re = lr * rr - li * ri
-                im = lr * ri + li * rr
-                sums[s] = re if j == 0 else sums[s] + re
-                sums[s + 4] = im if j == 0 else sums[s + 4] + im
+                for part in range(3):
+                    product = left_ref[pl.ds((now * 12 + part * 4 + s) * PAD + 8 * j, 8), :] * factors[part]
+                    at = part * 4 + s
+                    sums[at] = product if j == 0 else sums[at] + product
+        sums = [sums[8 + s] - sums[4 + s] for s in range(4)] + [sums[8 + s] + sums[s] for s in range(4)]
         tiles.append(fold(sums))
     return tiles
 
@@ -66,7 +66,7 @@
 
 
 def left_rows(left_ref, now, part, s, first, value):
-    left_ref[pl.ds((now * 8 + part * 4 + s) * PAD + first, value.shape[0]), :] = value
+    left_ref[pl.ds((now * 12 + part * 4 + s) * PAD + first, value.shape[0]), :] = value
 
 
 def dressed(left_ref, wide_ref, wilson, slices, now):
@@ -84,8 +84,10 @@
                 imag = im if imag is None else imag + im
             left_rows(left_ref, now, 0, s, b * 12, real)
             left_rows(left_ref, now, 1, s, b * 12, imag)
+            left_rows(left_ref, now, 2, s, b * 12, real + imag)
         left_rows(left_ref, now, 0, s, 36, zeros)
         left_rows(left_ref, now, 1, s, 36, zeros)
+        left_rows(left_ref, now, 2, s, 36, zeros)
 
 
 def fold(tiles):
@@ -168,6 +170,8 @@
             left_rows(plain_ref, now, 1, s, 0, -strided(wide_ref, 1, s, 0, 36, slices, now))
             left_rows(plain_ref, now, 0, s, 36, zeros)
             left_rows(plain_ref, now, 1, s, 36, zeros)
+            left_rows(plain_ref, now, 2, s, 36, zeros)
+            left_rows(plain_ref, now, 2, s, 0, strided(wide_ref, 0, s, 0, 36, slices, now) - strided(wide_ref, 1, s, 0, 36, slices, now))
         tiles = pair_rows(plain_ref, wide_ref, slices, now)
         for row in range(width // LANES):
             at = now * width + row * LANES
@@ -252,13 +256,13 @@
     linked = jnp.reshape(jnp.transpose(links, (1, 2, 3, 4, 0, 5)), (3, 3, slices, 2, sites))
     moved, moved_links = source, linked
     wide = pltpu.VMEM((288 * slices + 16 * slices, sites), f32)
-    plain = pltpu.VMEM((slices * 8 * PAD, sites), f32)
+    plain = pltpu.VMEM((slices * 12 * PAD, sites), f32)
     rows = -(-entries * 32 // LANES)
     width = rows * LANES
 
     moved = from_behind(moved, "gz", -1)
     chips, groups = chips_and_groups(sizes)
-    shape_left = kept((slices * 8 * PAD, sites))
+    shape_left = kept((slices * 12 * PAD, sites))
     shape_wilson = kept((slices * 18, sites))
     left, total, tables, wilson = pl.pallas_call(
         lambda *refs: first_kernel(slices, (slices_all, depth_count), scaling, entries, *refs),

time: 16.4 us -> 16.4 us (level)
  no operation moved by 1% of the time
where the time goes in v9:
time: 16.4 us; the launch traced here: 16.2 us
  blocking collectives  9.44 us (58%)
  starting transfers between devices  2.7 us (16%)
  Pallas kernels  2.56 us (16%)
  waiting for transfers between devices  1.53 us (9%)
    all_to_all x1, blocking collectives, body(): lax.all_to_all(jnp.reshape(total, (len(chips), 1, slices * width)), axes,...  9.44 us
    ppermute x1, starting transfers between devices, from_behind(): lax.ppermute(array, axis, [(i, (i + by) % peers) for i in range(peers)])  2.43 us
    pallas_call x1, Pallas kernels, body(): pl.pallas_call(lambda *refs: first_kernel(slices, (slices_all, depth_coun...  1.68 us
    ppermute x1, waiting for transfers between devices, body(): other = lax.ppermute(mine, 'gz', [(i, i ^ 1) for i in range(sizes[1])])  0.91 us
    pallas_call x1, Pallas kernels, body(): pl.pallas_call(lambda *refs: final_kernel(slices, results, [chip[0] for c...  0.69 us
    ppermute x1, waiting for transfers between devices, from_behind(): lax.ppermute(array, axis, [(i, (i + by) % peers) for i in range(peers)])  0.62 us
  transfers between devices with their start and end apart: 2, of which 2 were waited for; matrix products, arithmetic and copies ran while one was open for 0% of the time, Pallas kernels for 10%

profile of v9, /device:TPU:0, one launch (start us, length us, event | category | flops | bytes accessed | tf_op | source)
XLA Modules:
  0.0 16.2 jit_solution(4447529938769086928)
XLA Ops:
  0.0 2.4 %collective-permute-start = (bf16[288,128]{1,0:T(8,128)(2,1)}, bf16[288,128]{1,0:T(8,128)(2,1)S(1)}, u32[]{:S(2)}, u32[]{:S(2)}) collective-permute-start(bf16[288,128]{1,0:T(8,128)(2,1)} %bitcast.18), channel_id=1, source_target_pairs={{0,12},{4,0},{8,4},{12,8},{1,13},{5,1},{9,5},{13,9},{2,14},{6,2},{... | collective-permute-start | bytes 221192 | tf_op jit(solution)/shard_map/ppermute | solution.py:242
  2.4 1.7 %local.1 = (f32[480,128]{1,0:T(8,128)S(1)}, f32[1,128]{1,0:T(1,128)S(1)}, f32[32,128]{1,0:T(8,128)S(1)}, f32[18,128]{1,0:T(8,128)}) custom-call(s32[2,4]{1,0:T(2,128)} %refs_0_.1, s32[3]{0:T(128)} %refs_1_.1, s32[4]{0:T(128)} %refs_2_.1, s32[4,4]{1,0:T(4,128)} %refs_3_.1, s32[4,4]{1,0:T(4,128)} %refs_4_.1, bf16[288,128]{1,0:T(8,128)(2,1)} %bitcast.19, ...), custom_call_target="tpu_custom_call" | custom-call | tf_op jit(solution)/shard_map/local/pallas_call | solution.py:267
  4.1 0.6 %collective-permute-done.refs_1_ = bf16[288,128]{1,0:T(8,128)(2,1)S(1)} collective-permute-done((bf16[288,128]{1,0:T(8,128)(2,1)}, bf16[288,128]{1,0:T(8,128)(2,1)S(1)}, u32[]{:S(2)}, u32[]{:S(2)}) %collective-permute-start) | collective-permute-done | bytes 73760 | tf_op jit(solution)/shard_map/ppermute | solution.py:242
  4.7 0.2 %pairs.1 = f32[16,128]{1,0:T(8,128)S(1)} custom-call(f32[480,128]{1,0:T(8,128)S(1)} %get-tuple-element.8.refs_0_, bf16[288,128]{1,0:T(8,128)(2,1)S(1)} %collective-permute-done.refs_1_, f32[32,128]{1,0:T(8,128)S(1)} %get-tuple-element.9.refs_2_, f32[1,128]{1,0:T(1,128)S(1)} %get-tuple-element.10.refs_3_), custom_call_target="tpu_custom_call" | custom-call | tf_op jit(solution)/shard_map/pairs/pallas_call | solution.py:276
  4.9 9.4 %all_to_all.5 = f32[16,1,128]{2,1,0:T(1,128)S(1)} all-to-all(f32[16,1,128]{2,1,0:T(1,128)S(1)} %bitcast.17), channel_id=1, replica_groups={{27,19,26,18,25,17,24,16,11,3,10,2,9,1,8,0},{31,23,30,22,29,21,28,20,15..., dimensions={0} | all-to-all | bytes 16384 | tf_op jit(solution)/shard_map/all_to_all | solution.py:295
  14.4 0.3 %collective-permute-start.1 = (f32[16,128]{1,0:T(8,128)S(1)}, f32[16,128]{1,0:T(8,128)S(1)}, u32[]{:S(2)}, u32[]{:S(2)}) collective-permute-start(f32[16,128]{1,0:T(8,128)S(1)} %bitcast.15), channel_id=1, source_target_pairs={{0,4},{4,0},{8,12},{12,8},{1,5},{5,1},{9,13},{13,9},{2,6},{6,2},{1... | collective-permute-start | bytes 24584 | tf_op jit(solution)/shard_map/ppermute | solution.py:297
  14.6 0.9 %collective-permute-done.1.refs_1_ = f32[16,128]{1,0:T(8,128)S(1)} collective-permute-done((f32[16,128]{1,0:T(8,128)S(1)}, f32[16,128]{1,0:T(8,128)S(1)}, u32[]{:S(2)}, u32[]{:S(2)}) %collective-permute-start.1) | collective-permute-done | bytes 8224 | tf_op jit(solution)/shard_map/ppermute | solution.py:297
  15.5 0.7 %final.1 = f32[48,4]{1,0:T(8,128)} custom-call(f32[16,128]{1,0:T(8,128)S(1)} %bitcast.16, f32[16,128]{1,0:T(8,128)S(1)} %collective-permute-done.1.refs_1_), custom_call_target="tpu_custom_call" | custom-call | tf_op jit(solution)/shard_map/final/pallas_call | solution.py:299
Async XLA Ops:
  0.0 4.7 %collective-permute-start = (bf16[288,128]{1,0:T(8,128)(2,1)}, bf16[288,128]{1,0:T(8,128)(2,1)S(1)}, u32[]{:S(2)}, u32[]{:S(2)}) collective-permute-start(bf16[288,128]{1,0:T(8,128)(2,1)} %bitcast.18), channel_id=1, source_target_pairs={{0,12},{4,0},{8,4},{12,8},{1,13},{5,1},{9,5},{13,9},{2,14},{6,2},{... | collective-permute-start | bytes 221192 | tf_op jit(solution)/shard_map/ppermute | solution.py:242
  14.4 1.2 %collective-permute-start.1 = (f32[16,128]{1,0:T(8,128)S(1)}, f32[16,128]{1,0:T(8,128)S(1)}, u32[]{:S(2)}, u32[]{:S(2)}) collective-permute-start(f32[16,128]{1,0:T(8,128)S(1)} %bitcast.15), channel_id=1, source_target_pairs={{0,4},{4,0},{8,12},{12,8},{1,5},{5,1},{9,13},{13,9},{2,6},{6,2},{1... | collective-permute-start | bytes 24584 | tf_op jit(solution)/shard_map/ppermute | solution.py:297

commit v10 on v9

--- a/solution.py
+++ b/solution.py
@@ -231,9 +231,12 @@
 def chips_and_groups(sizes):
     nt, nz, ny = sizes
     chips = [(t, b, y) for t in range(nt) for b in range(nz // 2) for y in range(ny)]
-    corner = chips[-1]
-    chips.sort(key=lambda chip: (-chip[0], sum(abs(i - j) for i, j in zip(chip, corner)), chip))
-    groups = [[(t * nz + 2 * b + half) * ny + y for t, b, y in chips] for half in range(2)]
+    groups = []
+    for half in range(2):
+        t, b, y = max(chips)
+        leader = (t, b, max(y - half, 0))
+        chips.sort(key=lambda chip: (-chip[0], sum(abs(i - j) for i, j in zip(chip, leader)), chip))
+        groups.append([(t * nz + 2 * b + half) * ny + y for t, b, y in chips])
     return chips, groups
 
 

time: 16.4 us -> 16.4 us (level)
  no operation moved by 1% of the time
where the time goes in v10:
time: 16.4 us; the launch traced here: 16.2 us
  blocking collectives  9.44 us (58%)
  starting transfers between devices  2.61 us (16%)
  Pallas kernels  2.56 us (16%)
  waiting for transfers between devices  1.62 us (10%)
    all_to_all x1, blocking collectives, body(): lax.all_to_all(jnp.reshape(total, (len(chips), 1, slices * width)), axes,...  9.44 us
    ppermute x1, starting transfers between devices, from_behind(): lax.ppermute(array, axis, [(i, (i + by) % peers) for i in range(peers)])  2.43 us
    pallas_call x1, Pallas kernels, body(): pl.pallas_call(lambda *refs: first_kernel(slices, (slices_all, depth_coun...  1.68 us
    ppermute x1, waiting for transfers between devices, body(): other = lax.ppermute(mine, 'gz', [(i, i ^ 1) for i in range(sizes[1])])  1 us
    pallas_call x1, Pallas kernels, body(): pl.pallas_call(lambda *refs: final_kernel(slices, results, [chip[0] for c...  0.69 us
    ppermute x1, waiting for transfers between devices, from_behind(): lax.ppermute(array, axis, [(i, (i + by) % peers) for i in range(peers)])  0.62 us
  transfers between devices with their start and end apart: 2, of which 2 were waited for; matrix products, arithmetic and copies ran while one was open for 0% of the time, Pallas kernels for 10%

profile of v10, /device:TPU:0, one launch (start us, length us, event | category | flops | bytes accessed | tf_op | source)
XLA Modules:
  0.0 16.2 jit_solution(17386244901533902934)
XLA Ops:
  0.0 2.4 %collective-permute-start = (bf16[288,128]{1,0:T(8,128)(2,1)}, bf16[288,128]{1,0:T(8,128)(2,1)S(1)}, u32[]{:S(2)}, u32[]{:S(2)}) collective-permute-start(bf16[288,128]{1,0:T(8,128)(2,1)} %bitcast.18), channel_id=1, source_target_pairs={{0,12},{4,0},{8,4},{12,8},{1,13},{5,1},{9,5},{13,9},{2,14},{6,2},{... | collective-permute-start | bytes 221192 | tf_op jit(solution)/shard_map/ppermute | solution.py:245
  2.4 1.7 %local.1 = (f32[480,128]{1,0:T(8,128)S(1)}, f32[1,128]{1,0:T(1,128)S(1)}, f32[32,128]{1,0:T(8,128)S(1)}, f32[18,128]{1,0:T(8,128)}) custom-call(s32[2,4]{1,0:T(2,128)} %refs_0_.1, s32[3]{0:T(128)} %refs_1_.1, s32[4]{0:T(128)} %refs_2_.1, s32[4,4]{1,0:T(4,128)} %refs_3_.1, s32[4,4]{1,0:T(4,128)} %refs_4_.1, bf16[288,128]{1,0:T(8,128)(2,1)} %bitcast.19, ...), custom_call_target="tpu_custom_call" | custom-call | tf_op jit(solution)/shard_map/local/pallas_call | solution.py:270
  4.1 0.6 %collective-permute-done.refs_1_ = bf16[288,128]{1,0:T(8,128)(2,1)S(1)} collective-permute-done((bf16[288,128]{1,0:T(8,128)(2,1)}, bf16[288,128]{1,0:T(8,128)(2,1)S(1)}, u32[]{:S(2)}, u32[]{:S(2)}) %collective-permute-start) | collective-permute-done | bytes 73760 | tf_op jit(solution)/shard_map/ppermute | solution.py:245
  4.7 0.2 %pairs.1 = f32[16,128]{1,0:T(8,128)S(1)} custom-call(f32[480,128]{1,0:T(8,128)S(1)} %get-tuple-element.8.refs_0_, bf16[288,128]{1,0:T(8,128)(2,1)S(1)} %collective-permute-done.refs_1_, f32[32,128]{1,0:T(8,128)S(1)} %get-tuple-element.9.refs_2_, f32[1,128]{1,0:T(1,128)S(1)} %get-tuple-element.10.refs_3_), custom_call_target="tpu_custom_call" | custom-call | tf_op jit(solution)/shard_map/pairs/pallas_call | solution.py:279
  4.9 9.4 %all_to_all.5 = f32[16,1,128]{2,1,0:T(1,128)S(1)} all-to-all(f32[16,1,128]{2,1,0:T(1,128)S(1)} %bitcast.17), channel_id=1, replica_groups={{27,19,26,18,25,17,24,16,11,3,10,2,9,1,8,0},{30,22,29,31,21,23,28,20,14..., dimensions={0} | all-to-all | bytes 16384 | tf_op jit(solution)/shard_map/all_to_all | solution.py:298
  14.4 0.2 %collective-permute-start.1 = (f32[16,128]{1,0:T(8,128)S(1)}, f32[16,128]{1,0:T(8,128)S(1)}, u32[]{:S(2)}, u32[]{:S(2)}) collective-permute-start(f32[16,128]{1,0:T(8,128)S(1)} %bitcast.15), channel_id=1, source_target_pairs={{0,4},{4,0},{8,12},{12,8},{1,5},{5,1},{9,13},{13,9},{2,6},{6,2},{1... | collective-permute-start | bytes 24584 | tf_op jit(solution)/shard_map/ppermute | solution.py:300
  14.5 1.0 %collective-permute-done.1.refs_1_ = f32[16,128]{1,0:T(8,128)S(1)} collective-permute-done((f32[16,128]{1,0:T(8,128)S(1)}, f32[16,128]{1,0:T(8,128)S(1)}, u32[]{:S(2)}, u32[]{:S(2)}) %collective-permute-start.1) | collective-permute-done | bytes 8224 | tf_op jit(solution)/shard_map/ppermute | solution.py:300
  15.5 0.7 %final.1 = f32[48,4]{1,0:T(8,128)} custom-call(f32[16,128]{1,0:T(8,128)S(1)} %bitcast.16, f32[16,128]{1,0:T(8,128)S(1)} %collective-permute-done.1.refs_1_), custom_call_target="tpu_custom_call" | custom-call | tf_op jit(solution)/shard_map/final/pallas_call | solution.py:302
Async XLA Ops:
  0.0 4.7 %collective-permute-start = (bf16[288,128]{1,0:T(8,128)(2,1)}, bf16[288,128]{1,0:T(8,128)(2,1)S(1)}, u32[]{:S(2)}, u32[]{:S(2)}) collective-permute-start(bf16[288,128]{1,0:T(8,128)(2,1)} %bitcast.18), channel_id=1, source_target_pairs={{0,12},{4,0},{8,4},{12,8},{1,13},{5,1},{9,5},{13,9},{2,14},{6,2},{... | collective-permute-start | bytes 221192 | tf_op jit(solution)/shard_map/ppermute | solution.py:245
  14.4 1.2 %collective-permute-start.1 = (f32[16,128]{1,0:T(8,128)S(1)}, f32[16,128]{1,0:T(8,128)S(1)}, u32[]{:S(2)}, u32[]{:S(2)}) collective-permute-start(f32[16,128]{1,0:T(8,128)S(1)} %bitcast.15), channel_id=1, source_target_pairs={{0,4},{4,0},{8,12},{12,8},{1,5},{5,1},{9,13},{13,9},{2,6},{6,2},{1... | collective-permute-start | bytes 24584 | tf_op jit(solution)/shard_map/ppermute | solution.py:300
